TPU v7x, 512 devices: a whole 4x4x16 slice. The times are simulated.
512 devices in a mesh: dp: 32 (over x, y, core), expert: 16 (over z).
Axes of the slice: x: 4, y: 4, z: 16, core: 2. Of those that a mesh axis runs over, the one named last changes fastest.
Arguments:
- tokens: bfloat16 [131072, 1024], P(('dp', 'expert')), may hold values from -6 to 6
- grad_out: bfloat16 [131072, 1024], P(('dp', 'expert')), may hold values from -6 to 6
- expert_ids: int32 [131072, 8], P(('dp', 'expert')), may hold values from 0 to 127, all different within a row; in each aligned block of 256 rows (0 to 255, 256 to 511, ...) at most 32 rows name the same one
- router_weight: bfloat16 [1024, 128], replicated, may hold values from -0.1875 to 0.1875
- gate_weight_stack: bfloat16 [16, 1024, 384], P('expert'), may hold values from -0.1875 to 0.1875
- up_weight_stack: bfloat16 [16, 1024, 384], P('expert'), may hold values from -0.1875 to 0.1875
- down_weight_stack: bfloat16 [16, 384, 1024], P('expert'), may hold values from -0.3125 to 0.3125
Outputs:
- grad_tokens: bfloat16 [131072, 1024], P(('dp', 'expert'))
- grad_gate: float32 [16, 1024, 384], P('expert', 'dp')
- grad_up: float32 [16, 1024, 384], P('expert', 'dp')
- grad_down: float32 [16, 384, 1024], P('expert', 'dp')
- grad_router: float32 [1024, 128], replicated
Inputs may be any that keep to these rules, and one draw needn't show every extreme that they name: `expert_ids`: each row names 8 different experts; within the rows of one device (aligned blocks of 256 rows) no expert is named by more than 32 rows.
All inputs are finite; a program needn't handle non-finite values.
Results may differ from a plain program's by a relative error of at most 0.018.
Values may be sent and summed in bfloat16 or wider, within the bound.
A program may use at most 64 MiB of HBM per device.

v0:
```python
import math

import jax
import jax.numpy as jnp
from jax import lax
from jax.sharding import Mesh
from jax.sharding import PartitionSpec as P

DP = ("dp_0", "dp_1", "dp_2")
DP_EXPERT = ("dp_0", "dp_1", "dp_2", "expert")


def sent_together(arrays, axis, split_dim, concat_dim, along):
    widths = [math.prod(a.shape[along:]) for a in arrays]
    both = jnp.concatenate(
        [a.reshape(*a.shape[:along], w) for a, w in zip(arrays, widths)], axis=along
    )
    out = lax.all_to_all(both, axis, split_axis=split_dim, concat_axis=concat_dim, tiled=True)
    parts = jnp.split(out, [sum(widths[:k]) for k in range(1, len(widths))], axis=along)
    return tuple((b.reshape(*out.shape[:along], *a.shape[along:]) for a, b in zip(arrays, parts)))


def in_one_piece(arrays, axis, dim, along):
    widths = [a.shape[along] for a in arrays]
    both = jnp.concatenate(arrays, axis=along)
    out = lax.psum_scatter(both, axis, scatter_dimension=dim, tiled=True)
    return tuple(jnp.split(out, [sum(widths[:k]) for k in range(1, len(widths))], axis=along))


def in_blocks(value, dim, length):
    dims = value.shape
    parts = value.reshape(*dims[:dim], length, dims[dim] // length, *dims[dim + 1 :])
    return jnp.moveaxis(parts, dim, 0)


def sum_at_owner(value, axis, dim):
    length = lax.axis_size(axis)
    parts = lax.all_to_all(in_blocks(value, dim, length), axis, 0, 0, tiled=True)
    return jnp.sum(parts, axis=0)


def sum_by_axis(value, axes, dim):
    far, near = axes
    parts = in_blocks(value, dim, lax.axis_size(far))
    nearer = sum_at_owner(parts, near, dim + 1)
    arrived = lax.all_to_all(nearer, far, split_axis=0, concat_axis=0, tiled=True)
    return arrived.sum(axis=0)


def padded_to(lines, length):
    spare = -len(lines) % length
    return jnp.pad(lines, [(0, spare)] + [(0, 0)] * (lines.ndim - 1))


def copy_for_each(value, axis):
    length = lax.axis_size(axis)
    return lax.all_to_all(
        jnp.broadcast_to(value[None], (length, *value.shape)), axis, 0, 0, tiled=True
    )


def laid_out(parts, dim):
    dims = list(parts.shape[1:])
    dims[dim] *= parts.shape[0]
    return jnp.moveaxis(parts, 0, dim).reshape(dims)


def whole_of(value, axes, dim):
    far, near = axes
    initial = copy_for_each(value, far)
    parts = jnp.swapaxes(copy_for_each(initial, near), 0, 1)
    return laid_out(parts.reshape(-1, *value.shape), dim)


def total_of(value, axes):
    lines = value.reshape(-1, value.shape[-1])
    own = sum_by_axis(padded_to(lines, lax.axis_size(axes[0]) * lax.axis_size(axes[1])), axes, 0)
    whole = whole_of(own, axes, 0)
    return whole[: len(lines)].reshape(value.shape)


def to_experts(array, owners, flight_count):
    shaped = array.reshape((owners, flight_count, -1) + array.shape[2:])
    return jnp.swapaxes(shaped, 0, 1).reshape((flight_count, -1) + array.shape[2:])


def from_experts(array, owners, flight_count):
    shaped = array.reshape((flight_count, owners, -1) + array.shape[2:])
    return jnp.swapaxes(shaped, 0, 1).reshape((owners, -1) + array.shape[2:])


def local(
    tokens,
    grad_out,
    expert_ids,
    router_weight,
    gate_weight_stack,
    up_weight_stack,
    down_weight_stack,
):
    owners = lax.axis_size("expert")
    tok_count, model_width = tokens.shape
    top_count = expert_ids.shape[1]
    expert_count = router_weight.shape[1]
    flight_count = gate_weight_stack.shape[0]
    local_count = expert_count // owners
    capacity = tok_count // 8
    slot_count = flight_count * capacity
    route_count = tok_count * top_count
    logits = jnp.dot(tokens, router_weight, preferred_element_type=jnp.float32)
    expert_grid = lax.broadcasted_iota(jnp.int32, (1, 1, expert_count), 2)
    picked = expert_ids[:, :, None] == expert_grid
    chosen = jnp.sum(jnp.where(picked, logits[:, None, :], 0.0), axis=2)
    raised = jnp.exp(chosen)
    gate_values = raised / jnp.sum(raised, axis=1, keepdims=True)
    sent_gate = gate_values.astype(jnp.bfloat16).reshape(-1)
    local_index = expert_ids % local_count
    target = jnp.where(
        local_index < flight_count, expert_ids // local_count * flight_count + local_index, -1
    ).reshape(-1)
    columns = lax.broadcasted_iota(jnp.int32, (1, owners * flight_count), 1)
    onehot = (target[:, None] == columns).astype(jnp.int32)
    slot_rank = jnp.sum(onehot * (jnp.cumsum(onehot, axis=0) - 1), axis=1)
    position = jnp.where(target >= 0, target * capacity + slot_rank, owners * slot_count)
    route_ids = lax.iota(jnp.int32, route_count)
    slot_route = (
        jnp.full((owners * slot_count,), -1, jnp.int32).at[position].set(route_ids, mode="drop")
    )
    filled = slot_route >= 0
    safe_route = jnp.maximum(slot_route, 0)
    source_token = safe_route // top_count
    nothing = jnp.zeros((), jnp.bfloat16)
    send_tokens = jnp.where(filled[:, None], tokens[source_token], nothing).reshape(
        owners, slot_count, model_width
    )
    send_grads = jnp.where(filled[:, None], grad_out[source_token], nothing).reshape(
        owners, slot_count, model_width
    )
    send_gates = jnp.where(filled, sent_gate[safe_route], nothing).reshape(owners, slot_count)
    got_tokens, got_grads, got_gates = sent_together(
        (send_tokens, send_grads, send_gates), "expert", 0, 0, 2
    )
    expert_token_rows = to_experts(got_tokens, owners, flight_count)
    expert_grads = to_experts(got_grads, owners, flight_count)
    expert_gates = to_experts(got_gates, owners, flight_count)
    pre_gate = jnp.einsum(
        "uox,uxc->uoc", expert_token_rows, gate_weight_stack, preferred_element_type=jnp.float32
    )
    up_preactivation = jnp.einsum(
        "uox,uxc->uoc", expert_token_rows, up_weight_stack, preferred_element_type=jnp.float32
    )
    sigma = jax.nn.sigmoid(pre_gate)
    active_mask = (pre_gate * sigma * up_preactivation).astype(jnp.bfloat16)
    produced_rows = jnp.einsum(
        "zbp,zph->zbh", active_mask, down_weight_stack, preferred_element_type=jnp.float32
    )
    gate_grad = jnp.sum(expert_grads.astype(jnp.float32) * produced_rows, axis=2).astype(
        jnp.bfloat16
    )
    output_gradient = (
        expert_gates.astype(jnp.float32)[:, :, None] * expert_grads.astype(jnp.float32)
    ).astype(jnp.bfloat16)
    activation_gradient = jnp.einsum(
        "cnu,cyu->cny", output_gradient, down_weight_stack, preferred_element_type=jnp.float32
    )
    up_gradient = (activation_gradient * pre_gate * sigma).astype(jnp.bfloat16)
    gate_preactivation_gradient = (
        activation_gradient * up_preactivation * sigma * (1.0 + pre_gate * (1.0 - sigma))
    ).astype(jnp.bfloat16)
    token_grad = (
        jnp.einsum(
            "qza,qba->qzb",
            gate_preactivation_gradient,
            gate_weight_stack,
            preferred_element_type=jnp.float32,
        )
        + jnp.einsum(
            "qza,qba->qzb", up_gradient, up_weight_stack, preferred_element_type=jnp.float32
        )
    ).astype(jnp.bfloat16)
    back_tokens, back_gates = sent_together(
        (
            from_experts(token_grad, owners, flight_count),
            from_experts(gate_grad, owners, flight_count),
        ),
        "expert",
        0,
        0,
        2,
    )
    part_gate = jnp.einsum(
        "war,wak->wrk",
        expert_token_rows,
        gate_preactivation_gradient,
        preferred_element_type=jnp.float32,
    )
    partial_up_gradient = jnp.einsum(
        "war,wak->wrk", expert_token_rows, up_gradient, preferred_element_type=jnp.float32
    )
    partial_down_gradient = jnp.einsum(
        "xgr,xgn->xrn", active_mask, output_gradient, preferred_element_type=jnp.float32
    )
    grad_gate, grad_up, grad_down = (
        *tuple(
            (
                part.astype(jnp.float32)
                for part in in_one_piece(
                    (part_gate.astype(jnp.bfloat16), partial_up_gradient.astype(jnp.bfloat16)),
                    DP,
                    1,
                    0,
                )
            )
        ),
        lax.psum_scatter(
            partial_down_gradient.astype(jnp.bfloat16), DP, scatter_dimension=1, tiled=True
        ).astype(jnp.float32),
    )
    token_target = jnp.where(filled, source_token, tok_count)
    expert_part = (
        jnp.zeros((tok_count, model_width), jnp.float32)
        .at[token_target]
        .add(back_tokens.reshape(-1, model_width).astype(jnp.float32), mode="drop")
    )
    route_target = jnp.where(filled, slot_route, route_count)
    gate_grad_all = (
        jnp.zeros((route_count,), jnp.float32)
        .at[route_target]
        .add(back_gates.reshape(-1).astype(jnp.float32), mode="drop")
        .reshape(tok_count, top_count)
    )
    chosen_grad = gate_values * (
        gate_grad_all - jnp.sum(gate_values * gate_grad_all, axis=1, keepdims=True)
    )
    logit_grad = jnp.sum(jnp.where(picked, chosen_grad[:, :, None], 0.0), axis=1).astype(
        jnp.bfloat16
    )
    router_part = jnp.einsum("td,te->de", tokens, logit_grad, preferred_element_type=jnp.float32)
    grad_router = total_of(router_part, (("dp_0", "dp_1"), ("dp_2", "expert")))
    grad_tokens = (
        expert_part + jnp.dot(logit_grad, router_weight.T, preferred_element_type=jnp.float32)
    ).astype(jnp.bfloat16)
    return (grad_tokens, grad_gate, grad_up, grad_down, grad_router)


def solution(mesh):
    finer = Mesh(
        mesh.devices.reshape(4, 4, 2, mesh.shape["expert"]), ("dp_0", "dp_1", "dp_2", "expert")
    )
    return jax.shard_map(
        local,
        mesh=finer,
        in_specs=(
            P(DP_EXPERT, None),
            P(DP_EXPERT, None),
            P(DP_EXPERT, None),
            P(),
            P("expert", None, None),
            P("expert", None, None),
            P("expert", None, None),
        ),
        out_specs=(
            P(DP_EXPERT, None),
            P("expert", DP, None),
            P("expert", DP, None),
            P("expert", DP, None),
            P(),
        ),
        check_vma=False,
    )
```

profile of v0, /device:TPU:1, one launch (start us, length us, event | category | flops | bytes accessed | tf_op | source)
XLA Modules:
  0.0 429.0 jit_solution(5432786610859920385)
XLA Ops:
  7.2 0.8 broadcast_multiply_fusion
  8.7 4.5 %reduce-window.6 = s32[16,16,128]{2,1,0:T(8,128)S(1)} reduce-window(s32[16,16,128]{2,1,0:T(8,128)S(1)} %fusion.23, s32[]{:T(128)} %constant.60.clone.1), window={size=1x1x128 pad=0_0x0_0x127_0}, to_apply=%region_2.3 | reduce-window | flops 4161536 | bytes 262148 | tf_op jit(solution)/shard_map/reduce-window
  14.3 8.0 %scatter_custom_fusion = s32[512]{0:T(512)S(1)} fusion(s32[2048]{0:T(1024)S(1)} %bitcast.106, s32[2048]{0:T(1024)S(1)} %iota.17, s32[]{:T(128)} %constant.59.clone.1), kind=kCustom, calls=%fused_computation.92 | custom fusion | bytes 2052 | tf_op jit(solution)/shard_map/scatter | solution.py:127
  23.6 0.8 copy.68
  24.8 0.9 select_reduce_fusion.1
  26.0 3.5 gather_fusion.2
  29.8 2.1 gather_fusion
  31.9 2.8 gather_fusion.1
  34.7 1.4 broadcast_select_fusion.1
  36.3 117.0 %all_to_all.30 = bf16[16,32,2049]{2,1,0:T(8,128)(2,1)S(1)} all-to-all(bf16[16,32,2049]{2,1,0:T(8,128)(2,1)S(1)} %pad_maximum_fusion), channel_id=1, replica_groups=mesh['dp_0'=4,'dp_1'=4,'dp_2'=2,'expert'=16] {'expert'}, dimensions={0} | all-to-all | bytes 4196352 | tf_op jit(solution)/shard_map/all_to_all | solution.py:18
  153.3 1.4 copy-done.5
  155.0 1.8 fusion.38
  159.1 1.9 multiply_convert_fusion.2
  162.6 0.9 convert_element_type.193
  163.5 1.8 fusion.12
  166.4 62.8 %all_to_all.31 = bf16[16,32,1025]{2,1,0:T(8,128)(2,1)S(1)} all-to-all(bf16[16,32,1025]{2,1,0:T(8,128)(2,1)S(1)} %pad_maximum_fusion.2), channel_id=1, replica_groups=mesh['dp_0'=4,'dp_1'=4,'dp_2'=2,'expert'=16] {'expert'}, dimensions={0} | all-to-all | bytes 2099200 | tf_op jit(solution)/shard_map/all_to_all | solution.py:18
  229.2 1.0 copy-done.6
  231.0 3.7 scatter_custom_fusion.1
  235.5 1.1 multiply_reduce_fusion
  236.6 1.0 subtract_multiply_fusion
  237.6 2.1 select_reduce_fusion
  239.7 1.0 convolution_bitcast_fusion
  240.8 1.2 copy.75
  242.0 1.1 copy.76
  243.1 8.2 %all-to-all-start.2 = ((f32[32,16,2,128]{3,2,1,0:T(2,128)}), f32[32,16,2,128]{3,2,1,0:T(2,128)S(1)}, u32[]{:S(2)}, u32[]{:S(2)}) async-start(f32[32,16,2,128]{3,2,1,0:T(2,128)} %copy.76), calls=%async_computation.3 | async-start | bytes 1048576 | tf_op jit(solution)/shard_map/all_to_all | solution.py:38
  251.4 2.2 fusion.6
  254.3 1.3 pad_maximum_fusion.1
  255.7 25.9 %all-to-all-done.2 = f32[32,16,2,128]{3,2,1,0:T(2,128)S(1)} async-done(((f32[32,16,2,128]{3,2,1,0:T(2,128)}), f32[32,16,2,128]{3,2,1,0:T(2,128)S(1)}, u32[]{:S(2)}, u32[]{:S(2)}) %all-to-all-start.2) | async-done | bytes 524320 | tf_op jit(solution)/shard_map/all_to_all | solution.py:38
  281.8 13.0 %all_to_all.32 = f32[16,2,128]{2,1,0:T(2,128)S(1)} all-to-all(f32[16,2,128]{2,1,0:T(2,128)S(1)} %reduce_sum.81), channel_id=1, replica_groups=mesh['dp_0'=4,'dp_1'=4,'dp_2'=2,'expert'=16] {'dp_0','dp_1'}, dimensions={0} | all-to-all | bytes 32768 | tf_op jit(solution)/shard_map/all_to_all | solution.py:46
  294.8 9.5 %all_to_all.33 = f32[16,2,128]{2,1,0:T(2,128)S(1)} all-to-all(f32[16,2,128]{2,1,0:T(2,128)S(1)} %broadcast_in_dim.111), channel_id=1, replica_groups=mesh['dp_0'=4,'dp_1'=4,'dp_2'=2,'expert'=16] {'dp_0','dp_1'}, dimensions={0} | all-to-all | bytes 32768 | tf_op jit(solution)/shard_map/all_to_all | solution.py:57
  304.3 1.0 broadcast_in_dim.112
  305.4 8.6 %all-to-all-start.5 = ((f32[32,16,2,128]{3,2,1,0:T(2,128)}), f32[32,16,2,128]{3,2,1,0:T(2,128)S(1)}, u32[]{:S(2)}, u32[]{:S(2)}) async-start(f32[32,16,2,128]{3,2,1,0:T(2,128)} %broadcast_in_dim.112), calls=%async_computation.6 | async-start | bytes 1048576 | tf_op jit(solution)/shard_map/all_to_all | solution.py:57
  315.5 68.9 %fusion = bf16[16,1024]{1,0:T(8,128)(2,1)S(1)} fusion(bf16[1,384,1024]{2,1,0:T(8,128)(2,1)S(1)} %fusion.7), kind=kCustom, calls=%all-reduce-scatter | all-reduce-scatter fusion | flops 524289 | bytes 821248
  384.4 1.3 collective-permute-start.6
  385.7 1.3 collective-permute-start.5
  387.0 1.3 collective-permute-start.7
  388.3 1.3 collective-permute-start.4
  389.6 11.2 %collective-permute-start.3 = (bf16[16,1024]{1,0:T(8,128)(2,1)S(1)}, bf16[16,1024]{1,0:T(8,128)(2,1)S(1)}, u32[]{:S(2)}, u32[]{:S(2)}) collective-permute-start(bf16[16,1024]{1,0:T(8,128)(2,1)S(1)} %fusion), channel_id=1, source_target_pairs={{0,64},{16,80},{32,96},{48,112},{64,128},{80,144},{96,160},{112,17... | collective-permute-start | bytes 98312
  400.8 1.3 collective-permute-start.2
  402.2 4.0 collective-permute-start.1
  406.2 2.2 collective-permute-start
  408.4 1.3 dynamic-slice.4
  410.4 1.2 concatenate.12
  412.2 1.4 slice_convert_fusion.1
  413.6 1.2 fusion.40
  414.9 5.3 %scatter_custom_fusion.2 = f32[256,1024]{1,0:T(8,128)S(1)} fusion(f32[256,1024]{1,0:T(8,128)S(1)} %fusion.40, s32[512]{0:T(512)} %get-tuple-element.40, bf16[512,1024]{1,0:T(8,128)(2,1)S(1)} %bitcast.96), kind=kCustom, calls=%fused_computation.7 | custom fusion | flops 1048576 | bytes 2097152 | tf_op jit(solution)/shard_map/scatter-add | solution.py:223
  420.2 0.9 convert_element_type.177
  421.1 1.1 copy.78
  (91 shorter events, 13.9 us)
Async XLA Ops:
  7.2 149.7 %copy-start = (bf16[1,1024,384]{2,1,0:T(8,128)(2,1)S(1)}, bf16[1,1024,384]{2,1,0:T(8,128)(2,1)}, u32[]{:S(2)}) copy-start(bf16[1,1024,384]{2,1,0:T(8,128)(2,1)} %param.11) | copy-start | bytes 2359300
  7.2 17.3 %copy-start.1 = (bf16[256,1024]{1,0:T(8,128)(2,1)S(1)}, bf16[256,1024]{1,0:T(8,128)(2,1)}, u32[]{:S(2)}) copy-start(bf16[256,1024]{1,0:T(8,128)(2,1)} %param.7) | copy-start | bytes 1572868
  7.2 17.3 %copy-start.10 = (bf16[1024,128]{1,0:T(8,128)(2,1)S(1)}, bf16[1024,128]{1,0:T(8,128)(2,1)}, u32[]{:S(2)}) copy-start(bf16[1024,128]{1,0:T(8,128)(2,1)} %param.10) | copy-start | bytes 786436
  24.5 1.3 copy-start.9
  29.8 2.1 copy-start.2
  153.3 1.4 copy-start.5
  156.8 2.2 copy-start.3
  156.8 1.5 copy-start.7
  156.8 2.2 copy-start.11
  161.0 0.8 copy-start.13
  163.5 1.8 copy-start.8
  163.5 1.8 copy-start.16
  165.3 0.9 copy-start.12
  229.2 1.0 copy-start.6
  243.1 38.5 %all-to-all-start.2 = ((f32[32,16,2,128]{3,2,1,0:T(2,128)}), f32[32,16,2,128]{3,2,1,0:T(2,128)S(1)}, u32[]{:S(2)}, u32[]{:S(2)}) async-start(f32[32,16,2,128]{3,2,1,0:T(2,128)} %copy.76), calls=%async_computation.3 | async-start | bytes 1048576 | tf_op jit(solution)/shard_map/all_to_all | solution.py:38
  251.3 160.9 %reduce-scatter.5.cloned.1.call-start = ((), (), s32[]{:S(2)}) async-start(), calls=%async_computation.7 | async-start | bytes 1622016 | tf_op jit(solution)/shard_map/reduce_scatter | solution.py:26
  251.4 2.2 copy-start.4
  251.4 2.2 copy-start.15
  305.4 115.7 %all-to-all-start.5 = ((f32[32,16,2,128]{3,2,1,0:T(2,128)}), f32[32,16,2,128]{3,2,1,0:T(2,128)S(1)}, u32[]{:S(2)}, u32[]{:S(2)}) async-start(f32[32,16,2,128]{3,2,1,0:T(2,128)} %broadcast_in_dim.112), calls=%async_computation.6 | async-start | bytes 1048576 | tf_op jit(solution)/shard_map/all_to_all | solution.py:57
  313.9 1.0 copy-start.14
  384.4 17.7 %collective-permute-start.6 = (bf16[16,1024]{1,0:T(8,128)(2,1)S(1)}, bf16[16,1024]{1,0:T(8,128)(2,1)S(1)}, u32[]{:S(2)}, u32[]{:S(2)}) collective-permute-start(bf16[16,1024]{1,0:T(8,128)(2,1)S(1)} %fusion), channel_id=1, source_target_pairs={{0,112},{16,128},{32,144},{48,160},{64,176},{80,192},{96,208},{112... | collective-permute-start | bytes 98312
  385.7 20.5 %collective-permute-start.5 = (bf16[16,1024]{1,0:T(8,128)(2,1)S(1)}, bf16[16,1024]{1,0:T(8,128)(2,1)S(1)}, u32[]{:S(2)}, u32[]{:S(2)}) collective-permute-start(bf16[16,1024]{1,0:T(8,128)(2,1)S(1)} %fusion), channel_id=1, source_target_pairs={{0,96},{16,112},{32,128},{48,144},{64,160},{80,176},{96,192},{112,... | collective-permute-start | bytes 98312
  387.0 13.8 %collective-permute-start.7 = (bf16[12,1024]{1,0:T(8,128)(2,1)S(1)}, bf16[12,1024]{1,0:T(8,128)(2,1)S(1)}, u32[]{:S(2)}, u32[]{:S(2)}) collective-permute-start(bf16[12,1024]{1,0:T(8,128)(2,1)S(1)} %slice.16), channel_id=1, source_target_pairs={{0,128},{16,144},{32,160},{48,176},{64,192},{80,208},{96,224},{112... | collective-permute-start | bytes 73736
  388.3 22.0 %collective-permute-start.4 = (bf16[16,1024]{1,0:T(8,128)(2,1)S(1)}, bf16[16,1024]{1,0:T(8,128)(2,1)S(1)}, u32[]{:S(2)}, u32[]{:S(2)}) collective-permute-start(bf16[16,1024]{1,0:T(8,128)(2,1)S(1)} %fusion), channel_id=1, source_target_pairs={{0,80},{16,96},{32,112},{48,128},{64,144},{80,160},{96,176},{112,1... | collective-permute-start | bytes 98312
  389.6 20.7 %collective-permute-start.3 = (bf16[16,1024]{1,0:T(8,128)(2,1)S(1)}, bf16[16,1024]{1,0:T(8,128)(2,1)S(1)}, u32[]{:S(2)}, u32[]{:S(2)}) collective-permute-start(bf16[16,1024]{1,0:T(8,128)(2,1)S(1)} %fusion), channel_id=1, source_target_pairs={{0,64},{16,80},{32,96},{48,112},{64,128},{80,144},{96,160},{112,17... | collective-permute-start | bytes 98312
  400.8 9.5 %collective-permute-start.2 = (bf16[16,1024]{1,0:T(8,128)(2,1)S(1)}, bf16[16,1024]{1,0:T(8,128)(2,1)S(1)}, u32[]{:S(2)}, u32[]{:S(2)}) collective-permute-start(bf16[16,1024]{1,0:T(8,128)(2,1)S(1)} %fusion), channel_id=1, source_target_pairs={{0,48},{16,64},{32,80},{48,96},{64,112},{80,128},{96,144},{112,160... | collective-permute-start | bytes 98312
  402.2 8.2 %collective-permute-start.1 = (bf16[16,1024]{1,0:T(8,128)(2,1)S(1)}, bf16[16,1024]{1,0:T(8,128)(2,1)S(1)}, u32[]{:S(2)}, u32[]{:S(2)}) collective-permute-start(bf16[16,1024]{1,0:T(8,128)(2,1)S(1)} %fusion), channel_id=1, source_target_pairs={{0,32},{16,48},{32,64},{48,80},{64,96},{80,112},{96,128},{112,144}... | collective-permute-start | bytes 98312
  406.2 4.2 collective-permute-start
  410.3 4.6 %slice-start = ((bf16[16,32,1025]{2,1,0:T(8,128)(2,1)}), bf16[16,32,1024]{2,1,0:T(8,128)(2,1)S(1)}, s32[]{:S(2)}) async-start(bf16[16,32,1025]{2,1,0:T(8,128)(2,1)} %copy-done.6), calls=%async_computation.8 | async-start | bytes 2097152 | tf_op jit(solution)/shard_map/split | solution.py:19
Sparse Core Ops, SparseCore 0:
  256.6 100.8 reduce-scatter.4
where the time goes:
time: 430 us; the launch traced here: 429 us
  blocking collectives  271 us (63%)
  starting transfers between devices  40.7 us (9%)
  local copies, waits for them, and re-layouts  33.9 us (8%)
  other arithmetic  29.1 us (7%)
  waiting for transfers between devices  26 us (6%)
  between operations  15.4 us (4%)
  matrix products  12.8 us (3%)
    all_to_all x2, blocking collectives, sent_together(): lax.all_to_all(both, axis, split_axis=split_dim, concat_axis=concat_dim,...  180 us
    unnamed x1, blocking collectives  68.9 us
    all_to_all x1, waiting for transfers between devices, sum_at_owner(): lax.all_to_all(in_blocks(value, dim, length), axis, 0, 0, tiled=True)  25.9 us
    unnamed x8, starting transfers between devices  23.8 us
    all_to_all x1, blocking collectives, sum_by_axis(): lax.all_to_all(nearer, far, split_axis=0, concat_axis=0, tiled=True)  13 us
    all_to_all x1, blocking collectives, copy_for_each(): lax.all_to_all(jnp.broadcast_to(value[None], (length, *value.shape)), axi...  9.49 us
    unnamed x39, local copies, waits for them, and re-layouts  8.88 us
  transfers between devices with their start and end apart: 11, of which 1 were waited for; matrix products, arithmetic and copies ran while one was open for 20% of the time, Pallas kernels for 0%

commit v1 on v0

v1 whole, which is shorter than its diff:
```python
import functools

import jax
import jax.numpy as jnp
from jax import lax
from jax.experimental import pallas as pl
from jax.experimental.pallas import tpu as pltpu
from jax.sharding import Mesh
from jax.sharding import PartitionSpec as P

AX = ("dp_0", "dp_1", "dp_2", "expert")
MESH = pl.DeviceIdType.MESH
F32, BF16 = jnp.float32, jnp.bfloat16

NZ = 16
NCHIP = 16
CAP = 32
DIST = (-3, -2, -1, 0, 1, 2, 3, 4, -4)
RELATIVE = tuple(d % NZ for d in DIST) + tuple((d + 8) % NZ for d in DIST[:7])
NP, NS = 9, 7
HOME = 3
ORDER = (7, 8, 0, 6, 1, 5, 2, 4)


def wrap(v, n):
    return lax.rem(v + n, n)


def remote(src, dst, send, recv, **where):
    return pltpu.make_async_remote_copy(
        src_ref=src,
        dst_ref=dst,
        send_sem=send,
        recv_sem=recv,
        device_id={AX["xycz".index(k)]: v for k, v in where.items()},
        device_id_type=MESH,
    )


def place():
    return tuple(lax.axis_index(a) for a in AX)


def greet(partners):
    barrier = pltpu.get_barrier_semaphore()
    for where in partners:
        pl.semaphore_signal(
            barrier,
            inc=1,
            device_id={AX["xycz".index(k)]: v for k, v in where.items()},
            device_id_type=MESH,
        )
    pl.semaphore_wait(barrier, len(partners))


def plane_partners(x, y):
    return [
        dict(x=wrap(x + dx, 4), y=wrap(y + dy, 4))
        for dx in range(4)
        for dy in range(4)
        if dx or dy
    ]


def dispatch_kernel(
    st, sg, sgt, wg, wu, wd,
    ptok, stok, pgrad, sgrad, gts, w2g, w2u, w2d,
    t_send, t_recv, g_send, g_recv, gt_send, gt_recv,
    wz_send, wz_recv, wp_send, wp_recv, wc_send, wc_recv, loc,
):
    x, y, c, z = place()
    me = x * 4 + y
    other = 1 - c
    greet(
        [dict(z=wrap(z + d, NZ)) for d in (-4, -3, -2, -1, 1, 2, 3, 4, 8)]
        + plane_partners(x, y)
        + [dict(c=other)]
    )

    def piece(ref, m, core, chip):
        if m < 2:
            return ref.at[pl.ds(pl.multiple_of(512 * core + 32 * chip, 32), 32)]
        row = pl.multiple_of(192 * core + 48 * (chip // 4), 16)
        col = pl.multiple_of(256 * lax.rem(chip, 4), 128)
        return ref.at[pl.ds(row, 48), pl.ds(col, 256)]

    far = wrap(z + 8, NZ)
    own, second = (wg, wu, wd), (w2g, w2u, w2d)
    to_far = [
        remote(piece(own[m], m, c, me), piece(second[m], m, c, me), wz_send.at[m], wz_recv.at[m], z=far)
        for m in range(3)
    ]
    for cp in to_far:
        cp.start()

    sent = []
    for i in ORDER:
        to = wrap(z + DIST[i], NZ)
        sent.append(remote(sgt.at[i], gts.at[i], gt_send.at[i], gt_recv.at[i], z=to))
        sent.append(remote(st.at[i], ptok.at[i], t_send.at[i], t_recv.at[i], z=to))
        sent.append(remote(sg.at[i], pgrad.at[i], g_send.at[i], g_recv.at[i], z=to))
        if i < NS:
            j = NP + i
            sent.append(remote(st.at[j], stok.at[i], t_send.at[j], t_recv.at[j], z=to))
            sent.append(remote(sg.at[j], sgrad.at[i], g_send.at[j], g_recv.at[j], z=to))
    for cp in sent:
        cp.start()
    kept = [
        pltpu.make_async_copy(sgt.at[HOME], gts.at[HOME], loc.at[0]),
        pltpu.make_async_copy(st.at[HOME], ptok.at[HOME], loc.at[1]),
        pltpu.make_async_copy(sg.at[HOME], pgrad.at[HOME], loc.at[2]),
        pltpu.make_async_copy(st.at[NP + HOME], stok.at[HOME], loc.at[3]),
        pltpu.make_async_copy(sg.at[NP + HOME], sgrad.at[HOME], loc.at[4]),
    ]
    for cp in kept:
        cp.start()

    for cp in to_far:
        cp.wait_recv()

    def plane_copy(m, k):
        to = wrap(me + k, NCHIP)
        return remote(
            piece(second[m], m, c, me), piece(second[m], m, c, me),
            wp_send.at[m, k], wp_recv.at[m, k], x=to // 4, y=lax.rem(to, 4),
        )

    def arrived(m, k):
        frm = wrap(me - k + NCHIP, NCHIP)
        return remote(
            piece(second[m], m, c, frm), piece(second[m], m, c, frm),
            wp_send.at[m, k], wp_recv.at[m, k], x=frm // 4, y=lax.rem(frm, 4),
        )

    @pl.loop(1, NCHIP)
    def _(k):
        for m in range(3):
            plane_copy(m, k).start()

    @pl.loop(1, NCHIP)
    def _(k):
        for m in range(3):
            arrived(m, k).wait_recv()

    def half(ref, m):
        n = 512 if m < 2 else 192
        return ref.at[pl.ds(pl.multiple_of(n * c, n), n)]

    to_core = [
        remote(half(second[m], m), half(second[m], m), wc_send.at[m], wc_recv.at[m], c=other)
        for m in range(3)
    ]
    for cp in to_core:
        cp.start()
    for cp in to_far:
        cp.wait_send()

    @pl.loop(1, NCHIP)
    def _(k):
        for m in range(3):
            plane_copy(m, k).wait_send()

    for cp in to_core:
        cp.wait_send()
    for m in range(3):
        n = 512 if m < 2 else 192
        theirs = second[m].at[pl.ds(pl.multiple_of(n * other, n), n)]
        remote(theirs, theirs, wc_send.at[m], wc_recv.at[m], c=other).wait_recv()
    for cp in sent:
        cp.wait()
    for cp in kept:
        cp.wait()


def dispatch(st, sg, sgt, wg, wu, wd):
    hbm = pl.BlockSpec(memory_space=pl.ANY)
    dma = pltpu.SemaphoreType.DMA
    rows = lambda n: jax.ShapeDtypeStruct((n, CAP, 1024), BF16)
    return pl.pallas_call(
        dispatch_kernel,
        out_shape=(
            rows(NP), rows(NS), rows(NP), rows(NS),
            jax.ShapeDtypeStruct((NP, 8, 128), F32),
            jax.ShapeDtypeStruct(wg.shape, BF16),
            jax.ShapeDtypeStruct(wu.shape, BF16),
            jax.ShapeDtypeStruct(wd.shape, BF16),
        ),
        in_specs=[hbm] * 6,
        out_specs=(hbm,) * 8,
        scratch_shapes=[
            dma((16,)), dma((16,)), dma((16,)), dma((16,)), dma((9,)), dma((9,)),
            dma((3,)), dma((3,)), dma((3, 16)), dma((3, 16)), dma((3,)), dma((3,)), dma((5,)),
        ],
        compiler_params=pltpu.CompilerParams(collective_id=0, has_side_effects=True),
        name="dispatch",
    )(st, sg, sgt, wg, wu, wd)


def tail_kernel(
    oh, prob, tok, rw, prow, srow, gg,
    gp0, gp1, gp2, gs0, gs1, gs2,
    out_tok, out_w, out_r,
    rows_in, gg_in, sib, s0, rb, zs_out, zs_in, part, r_sib, r_half, r_in, r_z, r_zin, vbuf,
    row_send, row_recv, gg_send, gg_recv, sib_send, sib_recv, rs_send, rs_recv, zs_sem,
    r1_sem, r2_send, r2_recv, r3_send, r3_recv, r4_send, r4_recv, r5_send, r5_recv, r6_sem,
):
    x, y, c, z = place()
    me = x * 4 + y
    other = 1 - c
    far = wrap(z + 8, NZ)
    greet(
        [dict(z=wrap(z + d, NZ)) for d in range(1, NZ)]
        + plane_partners(x, y)
        + [dict(c=other)]
    )
    parts = (gp0, gp1, gp2, gs0, gs1, gs2)

    sent = [
        remote(gg.at[i], gg_in.at[i], gg_send.at[i], gg_recv.at[i], z=wrap(z - DIST[i] + NZ, NZ))
        for i in ORDER
    ]
    for cp in sent:
        cp.start()
    to_sib = [
        remote(parts[m].at[:, other], sib.at[m], sib_send.at[m], sib_recv.at[m], c=other)
        for m in range(6)
    ]
    for cp in to_sib:
        cp.start()
    rows = []
    for i in ORDER:
        to = wrap(z - DIST[i] + NZ, NZ)
        rows.append(remote(prow.at[i], rows_in.at[i], row_send.at[i], row_recv.at[i], z=to))
        if i < NS:
            j = NP + i
            rows.append(remote(srow.at[i], rows_in.at[j], row_send.at[j], row_recv.at[j], z=to))
    for cp in rows:
        cp.start()
    gg_in[HOME] = gg[HOME]
    rows_in[HOME] = prow[HOME]
    rows_in[NP + HOME] = srow[HOME]

    for cp in sent:
        cp.wait_recv()
    lane = lax.broadcasted_iota(jnp.int32, (CAP, 128), 1)
    sub = lax.broadcasted_iota(jnp.int32, (CAP, 128), 0)
    for g in range(16):
        i, s = (g, 0) if g < NP else (g - NP, 1)
        row = gg_in[i, s : s + 1, :]
        col = jnp.sum(jnp.where(lane == sub, row, 0.0), axis=1, keepdims=True)
        expert = 8 * lax.rem(z + RELATIVE[g], NZ)
        vbuf[g * CAP : (g + 1) * CAP, :] = jnp.where(lane == expert, col, 0.0).astype(BF16)
    grads = lax.dot_general(oh[...], vbuf[...], (((0,), (0,)), ((), ())), preferred_element_type=F32)
    p = prob[...]
    logit_grad = (p * (grads - jnp.sum(p * grads, axis=1, keepdims=True))).astype(BF16)
    part[...] = lax.dot_general(
        tok[...], logit_grad, (((0,), (0,)), ((), ())), preferred_element_type=F32
    ).reshape(part.shape)
    r1 = remote(part.at[other], r_sib, r1_sem.at[0], r1_sem.at[1], c=other)
    r1.start()

    def chip(k):
        to = wrap(me + k, NCHIP)
        return to, dict(x=to // 4, y=lax.rem(to, 4))

    r1.wait()
    r_half[...] = part[c] + r_sib[...]
    r_in[me] = r_half[me]

    def r2(k):
        to, where = chip(k)
        return remote(r_half.at[to], r_in.at[me], r2_send.at[k], r2_recv.at[k], **where)

    def r2_from(k):
        frm = wrap(me - k + NCHIP, NCHIP)
        return remote(r_half.at[0], r_in.at[frm], r2_send.at[k], r2_recv.at[k], x=frm // 4, y=lax.rem(frm, 4))

    @pl.loop(1, NCHIP)
    def _(k):
        r2(k).start()

    for cp in to_sib:
        cp.wait_recv()

    def rs(k):
        to, where = chip(k)
        return remote(s0.at[to], rb.at[me], rs_send.at[k], rs_recv.at[k], **where)

    def rs_from(k):
        frm = wrap(me - k + NCHIP, NCHIP)
        return remote(s0.at[0], rb.at[frm], rs_send.at[k], rs_recv.at[k], x=frm // 4, y=lax.rem(frm, 4))

    @pl.loop(1, NCHIP)
    def _(k):
        to, _w = chip(k)
        for m in range(6):
            s0[to, m] = (parts[m][to, c].astype(F32) + sib[m, to].astype(F32)).astype(BF16)
        rs(k).start()

    for m in range(6):
        rb[me, m] = (parts[m][me, c].astype(F32) + sib[m, me].astype(F32)).astype(BF16)

    @pl.loop(1, NCHIP)
    def _(k):
        r2_from(k).wait_recv()

    r_z[...] = jnp.sum(r_in[...], axis=0)

    def r3(k):
        to = wrap(z + k, NZ)
        return remote(r_z.at[to], r_zin.at[z], r3_send.at[k], r3_recv.at[k], z=to)

    def r3_from(k):
        frm = wrap(z - k + NZ, NZ)
        return remote(r_z.at[0], r_zin.at[frm], r3_send.at[k], r3_recv.at[k], z=frm)

    @pl.loop(1, NZ)
    def _(k):
        r3(k).start()

    r_zin[z] = r_z[z]

    for cp in rows:
        cp.wait_recv()
    out_tok[...] = (
        lax.dot_general(
            oh[...], rows_in[...].reshape(512, 1024), (((0,), (0,)), ((), ())), preferred_element_type=F32
        )
        + lax.dot_general(logit_grad, rw[...], (((1,), (1,)), ((), ())), preferred_element_type=F32)
    ).astype(BF16)

    @pl.loop(1, NZ)
    def _(k):
        r3_from(k).wait_recv()

    out_r[c, me, z] = jnp.sum(r_zin[...], axis=0)

    def r4(k):
        to = wrap(z + k, NZ)
        return remote(out_r.at[c, me, z], out_r.at[c, me, z], r4_send.at[k], r4_recv.at[k], z=to)

    def r4_from(k):
        frm = wrap(z - k + NZ, NZ)
        return remote(out_r.at[c, me, frm], out_r.at[c, me, frm], r4_send.at[k], r4_recv.at[k], z=frm)

    @pl.loop(1, NZ)
    def _(k):
        r4(k).start()

    @pl.loop(1, NZ)
    def _(k):
        r4_from(k).wait_recv()

    def r5(k):
        _to, where = chip(k)
        return remote(out_r.at[c, me], out_r.at[c, me], r5_send.at[k], r5_recv.at[k], **where)

    def r5_from(k):
        frm = wrap(me - k + NCHIP, NCHIP)
        return remote(out_r.at[c, frm], out_r.at[c, frm], r5_send.at[k], r5_recv.at[k], x=frm // 4, y=lax.rem(frm, 4))

    @pl.loop(1, NCHIP)
    def _(k):
        r5(k).start()

    @pl.loop(1, NCHIP)
    def _(k):
        rs_from(k).wait_recv()

    for m in range(3):
        zs_out[m] = jnp.sum(rb[:, 3 + m].astype(F32), axis=0).astype(BF16)
    zs = remote(zs_out, zs_in, zs_sem.at[0], zs_sem.at[1], z=far)
    zs.start()
    for m in range(3):
        out_w[m] = jnp.sum(rb[:, m].astype(F32), axis=0)

    @pl.loop(1, NCHIP)
    def _(k):
        r5_from(k).wait_recv()

    r6 = remote(out_r.at[c], out_r.at[c], r6_sem.at[0], r6_sem.at[1], c=other)
    r6.start()
    zs.wait()
    out_w[...] += zs_in[...].astype(F32)
    r6.wait_send()
    remote(out_r.at[other], out_r.at[other], r6_sem.at[0], r6_sem.at[1], c=other).wait_recv()
    for cp in sent + to_sib + rows:
        cp.wait_send()

    @pl.loop(1, NCHIP)
    def _(k):
        rs(k).wait_send()
        r2(k).wait_send()
        r3(k).wait_send()
        r4(k).wait_send()
        r5(k).wait_send()


def tail(oh, prob, tok, rw, prow, srow, gg, parts):
    vmem = pl.BlockSpec(memory_space=pltpu.VMEM)
    dma = pltpu.SemaphoreType.DMA
    V = pltpu.VMEM
    return pl.pallas_call(
        tail_kernel,
        out_shape=(
            jax.ShapeDtypeStruct((256, 1024), BF16),
            jax.ShapeDtypeStruct((3, 32, 384), F32),
            jax.ShapeDtypeStruct((2, 16, 16, 2, 128), F32),
        ),
        in_specs=[vmem] * 13,
        out_specs=(vmem,) * 3,
        scratch_shapes=[
            V((16, CAP, 1024), BF16), V((NP, 8, 128), F32),
            V((6, 16, 32, 384), BF16), V((16, 6, 32, 384), BF16), V((16, 6, 32, 384), BF16),
            V((3, 32, 384), BF16), V((3, 32, 384), BF16),
            V((2, 16, 16, 2, 128), F32), V((16, 16, 2, 128), F32), V((16, 16, 2, 128), F32),
            V((16, 16, 2, 128), F32), V((16, 2, 128), F32), V((16, 2, 128), F32),
            V((512, 128), BF16),
            dma((16,)), dma((16,)), dma((9,)), dma((9,)), dma((6,)), dma((6,)),
            dma((16,)), dma((16,)), dma((2,)),
            dma((2,)), dma((16,)), dma((16,)), dma((16,)), dma((16,)), dma((16,)), dma((16,)),
            dma((16,)), dma((16,)), dma((2,)),
        ],
        compiler_params=pltpu.CompilerParams(
            collective_id=1, has_side_effects=True, vmem_limit_bytes=48 << 20
        ),
        name="tail",
    )(oh, prob, tok, rw, prow, srow, gg, *parts)


def dot(a, b, ca, cb, out=F32):
    return lax.dot_general(a, b, (((ca,), (cb,)), ((), ())), preferred_element_type=out)


def expert(rows, grads, gates, wg, wu, wd):
    pre_gate = dot(rows, wg, 1, 0)
    pre_up = dot(rows, wu, 1, 0)
    sigma = jax.nn.sigmoid(pre_gate)
    active = (pre_gate * sigma * pre_up).astype(BF16)
    produced = dot(active, wd, 1, 0)
    gate_grad = jnp.sum(grads.astype(F32) * produced, axis=1).astype(BF16)
    out_grad = (gates[:, None] * grads.astype(F32)).astype(BF16)
    act_grad = dot(out_grad, wd, 1, 1)
    up_grad = (act_grad * pre_gate * sigma).astype(BF16)
    gate_pre = (act_grad * pre_up * sigma * (1.0 + pre_gate * (1.0 - sigma))).astype(BF16)
    back = (dot(gate_pre, wg, 1, 1) + dot(up_grad, wu, 1, 1)).astype(BF16)
    parts = (
        dot(rows, gate_pre, 0, 0).astype(BF16).reshape(16, 2, 32, 384),
        dot(rows, up_grad, 0, 0).astype(BF16).reshape(16, 2, 32, 384),
        dot(active, out_grad, 0, 0).astype(BF16).reshape(16, 2, 32, 384),
    )
    return back.reshape(-1, CAP, 1024), gate_grad.astype(F32), parts


def tiles(values):
    own = values[: NP * CAP].reshape(NP, 1, CAP)
    second = jnp.pad(values[NP * CAP :].reshape(NS, 1, CAP), ((0, NP - NS), (0, 0), (0, 0)))
    return jnp.pad(jnp.concatenate([own, second], axis=1), ((0, 0), (0, 6), (0, 128 - CAP)))


def local(tokens, grad_out, expert_ids, router_weight, wg, wu, wd):
    z = lax.axis_index("expert")
    wg, wu, wd = wg[0], wu[0], wd[0]
    experts = 8 * ((jnp.array(RELATIVE, jnp.int32) + z) % NZ)
    ids = expert_ids.T
    served = jnp.any(ids[:, None, :] == experts[None, :, None], axis=0)
    t = lax.broadcasted_iota(jnp.int32, (256, 256), 0)
    u = lax.broadcasted_iota(jnp.int32, (256, 256), 1)
    rank = dot(served.astype(BF16), (t < u).astype(BF16), 1, 0)
    slot = jnp.where(served, rank, -1.0)
    oh = (slot[:, None, :] == lax.broadcasted_iota(jnp.int32, (1, CAP, 1), 1).astype(F32)).astype(BF16)
    oh = oh.reshape(512, 256)
    logits = dot(tokens, router_weight, 1, 0)
    every = lax.broadcasted_iota(jnp.int32, (1, 1, 128), 2)
    mask = jnp.any(expert_ids[:, :, None] == every, axis=1)
    raised = jnp.where(mask, jnp.exp(logits), 0.0)
    prob = raised / jnp.sum(raised, axis=1, keepdims=True)
    slot_probs = dot(oh, prob.astype(BF16), 1, 0)
    at = jnp.repeat(experts, CAP)[:, None] == every[0]
    gates = jnp.sum(jnp.where(at, slot_probs, 0.0), axis=1)
    st = dot(oh, tokens, 1, 0, BF16).reshape(16, CAP, 1024)
    sg = dot(oh, grad_out, 1, 0, BF16).reshape(16, CAP, 1024)
    ptok, stok, pgrad, sgrad, gts, w2g, w2u, w2d = dispatch(st, sg, tiles(gates), wg, wu, wd)
    flat = lambda a: a.reshape(-1, 1024)
    prow, pgg, pparts = expert(flat(ptok), flat(pgrad), gts[:, 0, :CAP].reshape(-1), wg, wu, wd)
    srow, sgg, sparts = expert(flat(stok), flat(sgrad), gts[:NS, 1, :CAP].reshape(-1), w2g, w2u, w2d)
    grad_tokens, grads, router = tail(
        oh, prob, tokens, router_weight, prow, srow, tiles(jnp.concatenate([pgg, sgg])), pparts + sparts
    )
    return (
        grad_tokens,
        grads[0][None],
        grads[1][None],
        grads[2].reshape(1, 12, 1024),
        router.reshape(1024, 128),
    )


def solution(mesh):
    finer = Mesh(mesh.devices.reshape(4, 4, 2, NZ), AX)
    dp = AX[:3]
    return jax.shard_map(
        local,
        mesh=finer,
        in_specs=(
            P(AX, None), P(AX, None), P(AX, None), P(),
            P("expert", None, None), P("expert", None, None), P("expert", None, None),
        ),
        out_specs=(
            P(AX, None), P("expert", dp, None), P("expert", dp, None), P("expert", dp, None), P(),
        ),
        check_vma=False,
    )
```

time: 430 us -> 203 us (0.47)
  the two profiles are of different devices: /device:TPU:1 before, /device:TPU:60 now
where the time goes in v1:
time: 203 us; the launch traced here: 202 us
  Pallas kernels  150 us (74%)
  matrix products  28 us (14%)
  local copies, waits for them, and re-layouts  20.4 us (10%)
  other arithmetic  3.1 us (2%)
    pallas_call x1, Pallas kernels, tail(): pl.pallas_call(tail_kernel, out_shape=(jax.ShapeDtypeStruct((256, 1024),...  80.1 us
    pallas_call x1, Pallas kernels, dispatch(): pl.pallas_call(dispatch_kernel, out_shape=(rows(NP), rows(NS), rows(NP),...  69.6 us
    dot_general x23, matrix products, dot(): lax.dot_general(a, b, (((ca,), (cb,)), ((), ())), preferred_element_type=...  28 us
    unnamed x66, local copies, waits for them, and re-layouts  11.3 us
    reshape x2, local copies, waits for them, and re-layouts, expert(): dot(active, out_grad, 0, 0).astype(BF16).reshape(16, 2, 32, 384)  4.75 us

profile of v1, /device:TPU:60, one launch (start us, length us, event | category | flops | bytes accessed | tf_op | source)
XLA Modules:
  0.0 202.3 jit_solution(12849881074219550790)
XLA Ops:
  0.8 0.8 fusion.26
  1.5 0.8 compare_reduce_fusion
  2.6 0.8 copy.21
  3.5 0.4 fusion.6
  3.9 1.5 fusion.39
  5.5 1.5 fusion.10.st
  7.0 1.5 fusion.8.sg
  9.1 0.6 pad.18.sgt
  9.8 69.6 %dispatch.1 = (bf16[9,32,1024]{2,1,0:T(8,128)(2,1)}, bf16[7,32,1024]{2,1,0:T(8,128)(2,1)}, bf16[9,32,1024]{2,1,0:T(8,128)(2,1)}, bf16[7,32,1024]{2,1,0:T(8,128)(...) custom-call(bf16[16,32,1024]{2,1,0:T(8,128)(2,1)} %fusion.10.st, ...), custom_call_target="tpu_custom_call" | custom-call | tf_op jit(solution)/shard_map/dispatch/pallas_call | solution.py:179
  79.4 1.6 fusion.35
  81.0 0.8 slice_reduce_fusion.1
  82.0 0.5 fusion.28
  82.5 0.6 copy-done.15
  83.3 1.3 multiply_convert_fusion.3
  84.6 0.5 fusion.33
  85.3 0.5 fusion
  85.8 0.5 copy-done.10
  86.3 0.3 copy-done.13
  86.5 1.1 fusion.41
  87.7 0.8 slice_reduce_fusion
  88.5 1.8 fusion.20
  90.4 0.5 multiply_convert_fusion.6
  90.9 0.6 copy-done.14
  91.5 0.4 fusion.42
  92.0 0.4 fusion.1
  92.4 0.5 copy-done.16
  93.0 0.3 copy-done.18
  93.2 0.5 fusion.3
  93.8 1.8 fusion.2
  95.7 0.6 pad_convert_fusion.gg
  96.3 2.7 %convolution_convert_fusion.5 = bf16[1024,384]{1,0:T(8,128)(2,1)} fusion(bf16[288,1024]{1,0:T(8,128)(2,1)} %bitcast.96, bf16[288,384]{1,0:T(8,128)(2,1)} %copy-done.26), kind=kOutput, calls=%fused_computation.7 | convolution fusion | flops 226885632 | bytes 1597440 | tf_op jit(solution)/shard_map/dot_general | solution.py:432
  99.0 1.6 convolution_convert_fusion.4
  100.7 2.7 %convolution_convert_fusion.3 = bf16[384,1024]{1,0:T(8,128)(2,1)} fusion(bf16[288,384]{1,0:T(8,128)(2,1)} %get-tuple-element.42, f32[288]{0:T(512)S(1)} %mul.109, bf16[288,1024]{1,0:T(8,128)(2,1)} %bitcast.100), kind=kOutput, calls=%fused_computation.5 | convolution fusion | flops 227770368 | bytes 1598592 | tf_op jit(solution)/shard_map/dot_general | solution.py:432
  103.5 2.0 %reshape.151.gp2 = bf16[16,2,32,384]{3,2,1,0:T(8,128)(2,1)S(1)} reshape(bf16[384,1024]{1,0:T(8,128)(2,1)} %convolution_convert_fusion.3) | data formatting | bytes 1572864 | tf_op jit(solution)/shard_map/reshape | solution.py:450
  105.6 2.5 %convolution_convert_fusion.2 = bf16[1024,384]{1,0:T(8,128)(2,1)} fusion(bf16[224,1024]{1,0:T(8,128)(2,1)} %bitcast.83, bf16[224,384]{1,0:T(8,128)(2,1)S(1)} %get-tuple-element.46), kind=kOutput, calls=%fused_computation.4 | convolution fusion | flops 176553984 | bytes 1417216 | tf_op jit(solution)/shard_map/dot_general | solution.py:432
  108.0 1.4 convolution_convert_fusion.1
  109.4 1.3 convolution_convert_fusion
  110.8 2.7 %reshape.154.gs2 = bf16[16,2,32,384]{3,2,1,0:T(8,128)(2,1)} reshape(bf16[384,1024]{1,0:T(8,128)(2,1)} %convolution_convert_fusion) | data formatting | bytes 1572864 | tf_op jit(solution)/shard_map/reshape | solution.py:450
  113.5 1.1 copy-done.3
  114.6 1.1 copy-done.4
  115.8 0.8 copy-done.8
  116.5 80.1 %tail.1 = (bf16[256,1024]{1,0:T(8,128)(2,1)S(1)}, f32[3,32,384]{2,1,0:T(8,128)S(1)}, f32[2,16,16,2,128]{4,3,2,1,0:T(2,128)S(1)}) custom-call(bf16[512,256]{1,0:T(8,128)(2,1)S(1)} %get-tuple-element.54.oh, f32[256,128]{1,0:T(8,128)S(1)} %broadcast_divide_fusion.prob, bf16[256,1024]{1,0:T(8,128)(2,1)S(1)} %copy-done.1, bf16[1024,128]{1,0:T(8,128)(2,1)S(1)} %copy-done.2, ...), custom_call_target="tpu_custom_call" | custom-call | tf_op jit(solution)/shard_map/tail/pallas_call | solution.py:403
  196.7 0.8 copy-done.5
  197.5 0.8 copy-done.7
  198.3 0.6 fusion.38
  198.9 0.7 reshape_squeeze.4
  199.6 1.9 copy.34
  201.5 0.8 copy.35
  (71 shorter events, 2.1 us)
Async XLA Ops:
  0.6 6.4 %copy-start = (bf16[256,1024]{1,0:T(8,128)(2,1)S(1)}, bf16[256,1024]{1,0:T(8,128)(2,1)}, u32[]{:S(2)}) copy-start(bf16[256,1024]{1,0:T(8,128)(2,1)} %param.9) | copy-start | bytes 1572868
  0.6 4.9 %copy-start.1 = (bf16[256,1024]{1,0:T(8,128)(2,1)S(1)}, bf16[256,1024]{1,0:T(8,128)(2,1)}, u32[]{:S(2)}) copy-start(bf16[256,1024]{1,0:T(8,128)(2,1)} %tok.1) | copy-start | bytes 1572868
  9.7 69.6 %copy-start.9 = (bf16[1,1024,384]{2,1,0:T(8,128)(2,1)S(1)}, bf16[1,1024,384]{2,1,0:T(8,128)(2,1)}, u32[]{:S(2)}) copy-start(bf16[1,1024,384]{2,1,0:T(8,128)(2,1)} %param.12) | copy-start | bytes 2359300
  79.3 2.5 %copy-start.24 = (bf16[9,32,1024]{2,1,0:T(8,128)(2,1)S(1)}, bf16[9,32,1024]{2,1,0:T(8,128)(2,1)}, u32[]{:S(2)}) copy-start(bf16[9,32,1024]{2,1,0:T(8,128)(2,1)} %get-tuple-element.17) | copy-start | bytes 1769476
  79.4 2.7 %copy-start.12 = (bf16[1,384,1024]{2,1,0:T(8,128)(2,1)S(1)}, bf16[1,384,1024]{2,1,0:T(8,128)(2,1)}, u32[]{:S(2)}) copy-start(bf16[1,384,1024]{2,1,0:T(8,128)(2,1)} %param.14) | copy-start | bytes 2359300
  82.0 1.1 copy-start.15
  82.0 1.3 copy-start.22
  84.6 0.7 copy-start.26
  84.6 1.2 copy-start.27
  85.2 1.0 copy-start.10
  85.3 1.3 copy-start.13
  88.5 1.9 copy-start.19
  88.5 1.9 copy-start.25
  90.4 1.1 copy-start.14
  90.9 1.6 copy-start.20
  90.9 1.6 copy-start.29
  91.9 1.0 copy-start.16
  92.0 1.3 copy-start.18
  95.6 3.5 %copy-start.23 = (bf16[9,32,1024]{2,1,0:T(8,128)(2,1)S(1)}, bf16[9,32,1024]{2,1,0:T(8,128)(2,1)}, u32[]{:S(2)}) copy-start(bf16[9,32,1024]{2,1,0:T(8,128)(2,1)} %get-tuple-element.18) | copy-start | bytes 1769476
  95.7 3.4 %copy-start.28 = (bf16[288,384]{1,0:T(8,128)(2,1)S(1)}, bf16[288,384]{1,0:T(8,128)(2,1)}, u32[]{:S(2)}) copy-start(bf16[288,384]{1,0:T(8,128)(2,1)} %copy-done.27) | copy-start | bytes 663556
  105.5 2.5 %copy-start.11 = (bf16[7,32,1024]{2,1,0:T(8,128)(2,1)S(1)}, bf16[7,32,1024]{2,1,0:T(8,128)(2,1)}, u32[]{:S(2)}) copy-start(bf16[7,32,1024]{2,1,0:T(8,128)(2,1)} %get-tuple-element.21) | copy-start | bytes 1376260
  105.5 2.5 %copy-start.21 = (bf16[224,384]{1,0:T(8,128)(2,1)S(1)}, bf16[224,384]{1,0:T(8,128)(2,1)}, u32[]{:S(2)}) copy-start(bf16[224,384]{1,0:T(8,128)(2,1)} %copy-done.20) | copy-start | bytes 516100
  105.5 3.9 %copy-start.17 = (bf16[7,32,1024]{2,1,0:T(8,128)(2,1)S(1)}, bf16[7,32,1024]{2,1,0:T(8,128)(2,1)}, u32[]{:S(2)}) copy-start(bf16[7,32,1024]{2,1,0:T(8,128)(2,1)} %get-tuple-element.19) | copy-start | bytes 1376260
  105.6 3.9 %copy-start.30 = (bf16[224,384]{1,0:T(8,128)(2,1)S(1)}, bf16[224,384]{1,0:T(8,128)(2,1)}, u32[]{:S(2)}) copy-start(bf16[224,384]{1,0:T(8,128)(2,1)} %copy-done.29) | copy-start | bytes 516100
  109.4 4.1 %copy-start.2 = (bf16[1024,128]{1,0:T(8,128)(2,1)S(1)}, bf16[1024,128]{1,0:T(8,128)(2,1)}, u32[]{:S(2)}) copy-start(bf16[1024,128]{1,0:T(8,128)(2,1)} %rw.1) | copy-start | bytes 786436
  113.5 1.1 copy-start.3
  114.6 1.1 copy-start.4
  115.8 0.8 copy-start.8
  196.7 0.8 copy-start.5
  197.5 0.8 copy-start.7
  198.3 3.2 %copy-start.6 = (f32[2,16,16,2,128]{4,3,2,1,0:T(2,128)S(1)}, f32[2,16,16,2,128]{4,3,2,1,0:T(2,128)}, u32[]{:S(2)}) copy-start(f32[2,16,16,2,128]{4,3,2,1,0:T(2,128)} %copy-done.5) | copy-start | bytes 1572868

commit v2 on v1

v2 whole, which is shorter than its diff:
```python
import jax
import jax.numpy as jnp
from jax import lax
from jax.experimental import pallas as pl
from jax.experimental.pallas import tpu as pltpu
from jax.sharding import Mesh
from jax.sharding import PartitionSpec as P

AX = ("dp_0", "dp_1", "dp_2", "expert")
MESH = pl.DeviceIdType.MESH
F32, BF16 = jnp.float32, jnp.bfloat16

NZ = 16
NCHIP = 16
CAP = 32
DIST = (-3, -2, -1, 0, 1, 2, 3, 4, -4)
RELATIVE = tuple(d % NZ for d in DIST) + tuple((d + 8) % NZ for d in DIST[:7])
NP, NS = 9, 7
HOME = 3
ORDER = (7, 8, 0, 6, 1, 5, 2, 4)


def wrap(v, n):
    return lax.rem(v + n, n)


def at(where):
    return {AX["xycz".index(k)]: v for k, v in where.items()}


def remote(src, dst, send, recv, **where):
    return pltpu.make_async_remote_copy(
        src_ref=src, dst_ref=dst, send_sem=send, recv_sem=recv, device_id=at(where), device_id_type=MESH
    )


def dot(a, b, ca, cb):
    return lax.dot_general(a, b, (((ca,), (cb,)), ((), ())), preferred_element_type=F32)


def starts(copies):
    for cp in copies:
        cp.start()


def whole(
    tok_h, grad_h, ids_h, rw_h, wg_h, wu_h, wd_h,
    out_tok, out_w, out_d, out_r,
    tok, grad, ids, rw, w1, w1d, w2, w2d,
    oh, prob, st, sg, sgt, sel,
    ptok, stok, pgrad, sgrad, gts,
    pre, act, og, gu, ac, made,
    prow, srow, gg, rows_in, gg_in, vbuf,
    pa, pd, sa, sd, sib_pa, sib_pd, sib_sa, sib_sd,
    s_pa, s_pd, s_sa, s_sd, rb_pa, rb_pd, rb_sa, rb_sd,
    za_out, zd_out, za_in, zd_in,
    part, r_sib, r_half, r_in, r_z, r_zin,
    loc, t_send, t_recv, g_send, g_recv, gt_send, gt_recv,
    wz_send, wz_recv, wp_send, wp_recv, wc_send, wc_recv,
    row_send, row_recv, gg_send, gg_recv,
    sib_send, sib_recv, rs_send, rs_recv, zs_sem,
    r1_sem, r2_send, r2_recv, r3_send, r3_recv, r4_send, r4_recv, r5_send, r5_recv, r6_sem,
):
    x, y, c, z = tuple(lax.axis_index(a) for a in AX)
    me = x * 4 + y
    other = 1 - c
    far = wrap(z + 8, NZ)

    fetch = [
        pltpu.make_async_copy(ids_h, ids, loc.at[0]),
        pltpu.make_async_copy(tok_h, tok, loc.at[1]),
        pltpu.make_async_copy(rw_h, rw, loc.at[2]),
        pltpu.make_async_copy(grad_h, grad, loc.at[3]),
        pltpu.make_async_copy(wg_h, w1.at[:, pl.ds(0, 384)], loc.at[4]),
        pltpu.make_async_copy(wu_h, w1.at[:, pl.ds(384, 384)], loc.at[5]),
        pltpu.make_async_copy(wd_h, w1d, loc.at[6]),
    ]
    starts(fetch)

    barrier = pltpu.get_barrier_semaphore()
    partners = [dict(z=wrap(z + d, NZ)) for d in range(1, NZ)] + [dict(c=other)]
    partners += [
        dict(x=wrap(x + dx, 4), y=wrap(y + dy, 4)) for dx in range(4) for dy in range(4) if dx or dy
    ]
    for where in partners:
        pl.semaphore_signal(barrier, inc=1, device_id=at(where), device_id_type=MESH)

    def chip(k):
        to = wrap(me + k, NCHIP)
        return to, dict(x=to // 4, y=lax.rem(to, 4))

    def chip_from(k):
        frm = wrap(me - k + NCHIP, NCHIP)
        return frm, dict(x=frm // 4, y=lax.rem(frm, 4))

    lane = lax.broadcasted_iota(jnp.int32, (CAP, 128), 1)
    sub = lax.broadcasted_iota(jnp.int32, (CAP, 128), 0)

    def expert_of(g):
        return 8 * lax.rem(z + RELATIVE[g], NZ)

    def to_row(col):
        return jnp.sum(jnp.where(lane == sub, col, 0.0), axis=0, keepdims=True)

    def to_col(row):
        return jnp.sum(jnp.where(lane == sub, row, 0.0), axis=1, keepdims=True)

    fetch[0].wait()
    every = lax.broadcasted_iota(jnp.int32, (256, 128), 1)
    named = ids[:, 0:1] == every
    for k in range(1, 8):
        named = jnp.logical_or(named, ids[:, k : k + 1] == every)
    mask = jnp.where(named, 1.0, 0.0).astype(BF16)
    row16 = lax.broadcasted_iota(jnp.int32, (16, 128), 0)
    rel = jnp.zeros((16, 128), jnp.int32)
    for g in range(16):
        rel = jnp.where(row16 == g, expert_of(g), rel)
    mine = jnp.where(lax.broadcasted_iota(jnp.int32, (16, 128), 1) == rel, 1.0, 0.0).astype(BF16)
    served = dot(mine, mask, 1, 1)
    before = lax.broadcasted_iota(jnp.int32, (256, 256), 0) < lax.broadcasted_iota(jnp.int32, (256, 256), 1)
    rank = dot(served.astype(BF16), jnp.where(before, 1.0, 0.0).astype(BF16), 1, 0)
    slot = jnp.where(served > 0.5, rank, -1.0)
    want = lax.broadcasted_iota(jnp.int32, (CAP, 256), 0).astype(F32)
    for g in range(16):
        oh[g * CAP : (g + 1) * CAP, :] = jnp.where(slot[g : g + 1, :] == want, 1.0, 0.0).astype(BF16)
    fetch[1].wait()
    st[...] = dot(oh[...], tok[...], 1, 0).astype(BF16).reshape(st.shape)
    fetch[2].wait()
    logits = dot(tok[...], rw[...], 1, 0)
    raised = jnp.where(named, jnp.exp(logits), 0.0)
    prob[...] = raised / jnp.sum(raised, axis=1, keepdims=True)
    slot_prob = dot(oh[...], prob[...].astype(BF16), 1, 0)
    sgt[...] = jnp.zeros_like(sgt)
    for g in range(16):
        i, s = (g, 0) if g < NP else (g - NP, 1)
        col = jnp.sum(
            jnp.where(lane == expert_of(g), slot_prob[g * CAP : (g + 1) * CAP, :], 0.0), axis=1, keepdims=True
        )
        sgt[i, s : s + 1, :] = to_row(col)
    fetch[3].wait()
    sg[...] = dot(oh[...], grad[...], 1, 0).astype(BF16).reshape(sg.shape)
    for cp in fetch[4:]:
        cp.wait()

    pl.semaphore_wait(barrier, len(partners))

    def piece(ref, m, core, p):
        if m == 0:
            return ref.at[pl.ds(pl.multiple_of(512 * core + 32 * p, 32), 32)]
        row = pl.multiple_of(192 * core + 48 * (p // 4), 16)
        col = pl.multiple_of(256 * lax.rem(p, 4), 128)
        return ref.at[pl.ds(row, 48), pl.ds(col, 256)]

    own, second = (w1, w1d), (w2, w2d)
    to_far = [
        remote(piece(own[m], m, c, me), piece(second[m], m, c, me), wz_send.at[m], wz_recv.at[m], z=far)
        for m in range(2)
    ]
    starts(to_far)

    first, later = [], []
    for i in ORDER:
        to = wrap(z + DIST[i], NZ)
        first.append(remote(sgt.at[i], gts.at[i], gt_send.at[i], gt_recv.at[i], z=to))
        first.append(remote(st.at[i], ptok.at[i], t_send.at[i], t_recv.at[i], z=to))
        first.append(remote(sg.at[i], pgrad.at[i], g_send.at[i], g_recv.at[i], z=to))
        if i < NS:
            j = NP + i
            later.append(remote(st.at[j], stok.at[i], t_send.at[j], t_recv.at[j], z=to))
            later.append(remote(sg.at[j], sgrad.at[i], g_send.at[j], g_recv.at[j], z=to))
    starts(first)
    starts(later)
    gts[HOME] = sgt[HOME]
    ptok[HOME] = st[HOME]
    pgrad[HOME] = sg[HOME]
    stok[HOME] = st[NP + HOME]
    sgrad[HOME] = sg[NP + HOME]

    q = lax.broadcasted_iota(jnp.int32, (384, 512), 1)
    unit = lax.broadcasted_iota(jnp.int32, (384, 512), 0)
    block, k16 = q // 16, lax.rem(q, 16)
    sel[...] = jnp.where(jnp.logical_and(unit == block * 12 + k16, k16 < 12), 1.0, 0.0).astype(BF16)

    for cp in to_far:
        cp.wait_recv()

    def plane_copy(m, k):
        _to, where = chip(k)
        mine_ = piece(second[m], m, c, me)
        return remote(mine_, mine_, wp_send.at[m, k], wp_recv.at[m, k], **where)

    def plane_from(m, k):
        frm, where = chip_from(k)
        theirs = piece(second[m], m, c, frm)
        return remote(theirs, theirs, wp_send.at[m, k], wp_recv.at[m, k], **where)

    @pl.loop(1, NCHIP)
    def _(k):
        for m in range(2):
            plane_copy(m, k).start()

    @pl.loop(1, NCHIP)
    def _(k):
        for m in range(2):
            plane_from(m, k).wait_recv()

    def half(m, core):
        n = 512 if m == 0 else 192
        ref = second[m].at[pl.ds(pl.multiple_of(n * core, n), n)]
        return remote(ref, ref, wc_send.at[m], wc_recv.at[m], c=other)

    for m in range(2):
        half(m, c).start()

    def expert_rows(n, rows, grads, s, w, wd):
        m = n * CAP

        @pl.loop(0, n)
        def _(g):
            og[g] = (to_col(gts[g, s : s + 1, :]) * grads[g].astype(F32)).astype(BF16)

        pre[0:n] = dot(rows[...].reshape(m, 1024), w[...], 1, 0).reshape(n, CAP, 768)
        act[0:n] = dot(og[0:n].reshape(m, 1024), wd[...], 1, 1).reshape(n, CAP, 384)

        @pl.loop(0, n)
        def _(g):
            pg, pu, ag = pre[g, :, 0:384], pre[g, :, 384:768], act[g]
            sigma = lax.logistic(pg)
            ac[g] = (pg * sigma * pu).astype(BF16)
            gu[g, :, 0:384] = (ag * pu * sigma * (1.0 + pg * (1.0 - sigma))).astype(BF16)
            gu[g, :, 384:768] = (ag * pg * sigma).astype(BF16)

    def expert_parts(n, rows, a, d):
        m = n * CAP
        a[...] = dot(rows[...].reshape(m, 1024), gu[0:n].reshape(m, 768), 0, 0).astype(BF16).reshape(a.shape)
        spread = dot(ac[0:n].reshape(m, 384), sel[...], 1, 0).astype(BF16)
        d[...] = dot(spread, og[0:n].reshape(m, 1024), 0, 0).astype(BF16).reshape(d.shape)

    def expert_gates(n, grads, s, wd):
        m = n * CAP
        made[0:n] = dot(ac[0:n].reshape(m, 384), wd[...], 1, 0).reshape(n, CAP, 1024)

        @pl.loop(0, n)
        def _(g):
            col = jnp.sum(grads[g].astype(F32) * made[g], axis=1, keepdims=True)
            gg[g, s] = to_row(col.astype(BF16).astype(F32))

    def expert_back(n, w, back):
        m = n * CAP
        back[...] = dot(gu[0:n].reshape(m, 768), w[...], 1, 1).astype(BF16).reshape(back.shape)

    def give_gates(s, n):
        return [
            remote(gg.at[i, s], gg_in.at[i, s], gg_send.at[s, i], gg_recv.at[s, i], z=wrap(z - DIST[i] + NZ, NZ))
            for i in ORDER
            if i < n
        ]

    def give_rows(back, n, base):
        return [
            remote(back.at[i], rows_in.at[base + i], row_send.at[base + i], row_recv.at[base + i], z=wrap(z - DIST[i] + NZ, NZ))
            for i in ORDER
            if i < n
        ]

    def swap_core(a, d, a_in, d_in, e):
        return [
            remote(a.at[:, other], a_in, sib_send.at[e, 0], sib_recv.at[e, 0], c=other),
            remote(d.at[:, other], d_in, sib_send.at[e, 1], sib_recv.at[e, 1], c=other),
        ]

    def add_core(a, d, a_in, d_in, s_a, s_d):
        @pl.loop(0, NCHIP)
        def _(k):
            s_a[k] = (a[k, c].astype(F32) + a_in[k].astype(F32)).astype(BF16)
            s_d[k] = (d[k, c].astype(F32) + d_in[k].astype(F32)).astype(BF16)

    def scatter(e, k, s_a, s_d, rb_a, rb_d):
        to, where = chip(k)
        return [
            remote(s_a.at[to], rb_a.at[me], rs_send.at[e, 0, k], rs_recv.at[e, 0, k], **where),
            remote(s_d.at[to], rb_d.at[me], rs_send.at[e, 1, k], rs_recv.at[e, 1, k], **where),
        ]

    def scattered(e, k, s_a, s_d, rb_a, rb_d):
        frm, where = chip_from(k)
        return [
            remote(s_a.at[0], rb_a.at[frm], rs_send.at[e, 0, k], rs_recv.at[e, 0, k], **where),
            remote(s_d.at[0], rb_d.at[frm], rs_send.at[e, 1, k], rs_recv.at[e, 1, k], **where),
        ]

    for cp in first:
        cp.wait_recv()
    expert_rows(NP, ptok, pgrad, 0, w1, w1d)
    expert_parts(NP, ptok, pa, pd)
    swap_p = swap_core(pa, pd, sib_pa, sib_pd, 0)
    starts(swap_p)
    expert_gates(NP, pgrad, 0, w1d)
    gates_p = give_gates(0, NP)
    starts(gates_p)
    expert_back(NP, w1, prow)
    rows_p = give_rows(prow, NP, 0)
    starts(rows_p)
    rows_in[HOME] = prow[HOME]
    gg_in[HOME, 0] = gg[HOME, 0]
    for cp in swap_p:
        cp.wait_recv()
    add_core(pa, pd, sib_pa, sib_pd, s_pa, s_pd)
    arrays_p = (s_pa, s_pd, rb_pa, rb_pd)

    @pl.loop(1, NCHIP)
    def _(k):
        starts(scatter(0, k, *arrays_p))

    rb_pa[me] = s_pa[me]
    rb_pd[me] = s_pd[me]

    for m in range(2):
        half(m, other).wait_recv()
    for cp in later:
        cp.wait_recv()
    expert_rows(NS, stok, sgrad, 1, w2, w2d)
    expert_gates(NS, sgrad, 1, w2d)
    gates_s = give_gates(1, NS)
    starts(gates_s)
    expert_parts(NS, stok, sa, sd)
    swap_s = swap_core(sa, sd, sib_sa, sib_sd, 1)
    starts(swap_s)
    expert_back(NS, w2, srow)
    rows_s = give_rows(srow, NS, NP)
    starts(rows_s)
    rows_in[NP + HOME] = srow[HOME]
    gg_in[HOME, 1] = gg[HOME, 1]

    for cp in gates_p + gates_s:
        cp.wait_recv()
    for g in range(16):
        i, s = (g, 0) if g < NP else (g - NP, 1)
        col = to_col(gg_in[i, s])
        vbuf[g * CAP : (g + 1) * CAP, :] = jnp.where(lane == expert_of(g), col, 0.0).astype(BF16)
    grads = dot(oh[...], vbuf[...], 0, 0)
    p = prob[...]
    logit_grad = (p * (grads - jnp.sum(p * grads, axis=1, keepdims=True))).astype(BF16)
    part[...] = dot(tok[...], logit_grad, 0, 0).reshape(part.shape)
    r1 = remote(part.at[other], r_sib, r1_sem.at[0], r1_sem.at[1], c=other)
    r1.start()
    for cp in swap_s:
        cp.wait_recv()
    add_core(sa, sd, sib_sa, sib_sd, s_sa, s_sd)
    arrays_s = (s_sa, s_sd, rb_sa, rb_sd)
    r1.wait()
    r_half[...] = part[c] + r_sib[...]
    r_in[me] = r_half[me]

    def r2(k):
        to, where = chip(k)
        return remote(r_half.at[to], r_in.at[me], r2_send.at[k], r2_recv.at[k], **where)

    def r2_from(k):
        frm, where = chip_from(k)
        return remote(r_half.at[0], r_in.at[frm], r2_send.at[k], r2_recv.at[k], **where)

    @pl.loop(1, NCHIP)
    def _(k):
        r2(k).start()

    @pl.loop(1, NCHIP)
    def _(k):
        starts(scatter(1, k, *arrays_s))

    rb_sa[me] = s_sa[me]
    rb_sd[me] = s_sd[me]

    @pl.loop(1, NCHIP)
    def _(k):
        r2_from(k).wait_recv()

    r_z[...] = jnp.sum(r_in[...], axis=0)

    def r3(k):
        return remote(r_z.at[wrap(z + k, NZ)], r_zin.at[z], r3_send.at[k], r3_recv.at[k], z=wrap(z + k, NZ))

    def r3_from(k):
        frm = wrap(z - k + NZ, NZ)
        return remote(r_z.at[0], r_zin.at[frm], r3_send.at[k], r3_recv.at[k], z=frm)

    @pl.loop(1, NZ)
    def _(k):
        r3(k).start()

    r_zin[z] = r_z[z]

    for cp in rows_p + rows_s:
        cp.wait_recv()
    out_tok[...] = (
        dot(oh[...], rows_in[...].reshape(512, 1024), 0, 0) + dot(logit_grad, rw[...], 1, 1)
    ).astype(BF16)

    @pl.loop(1, NZ)
    def _(k):
        r3_from(k).wait_recv()

    out_r[c, me, z] = jnp.sum(r_zin[...], axis=0)

    def r4(k):
        ref = out_r.at[c, me, z]
        return remote(ref, ref, r4_send.at[k], r4_recv.at[k], z=wrap(z + k, NZ))

    def r4_from(k):
        frm = wrap(z - k + NZ, NZ)
        ref = out_r.at[c, me, frm]
        return remote(ref, ref, r4_send.at[k], r4_recv.at[k], z=frm)

    @pl.loop(1, NZ)
    def _(k):
        r4(k).start()

    @pl.loop(1, NCHIP)
    def _(k):
        for cp in scattered(0, k, *arrays_p):
            cp.wait_recv()

    out_w[...] = jnp.sum(rb_pa[...].astype(F32), axis=0)
    out_d[...] = jnp.sum(rb_pd[...].astype(F32), axis=0)

    @pl.loop(1, NZ)
    def _(k):
        r4_from(k).wait_recv()

    def r5(k):
        _to, where = chip(k)
        ref = out_r.at[c, me]
        return remote(ref, ref, r5_send.at[k], r5_recv.at[k], **where)

    def r5_from(k):
        frm, where = chip_from(k)
        ref = out_r.at[c, frm]
        return remote(ref, ref, r5_send.at[k], r5_recv.at[k], **where)

    @pl.loop(1, NCHIP)
    def _(k):
        r5(k).start()

    @pl.loop(1, NCHIP)
    def _(k):
        for cp in scattered(1, k, *arrays_s):
            cp.wait_recv()

    za_out[...] = jnp.sum(rb_sa[...].astype(F32), axis=0).astype(BF16)
    zd_out[...] = jnp.sum(rb_sd[...].astype(F32), axis=0).astype(BF16)
    zs = [
        remote(za_out, za_in, zs_sem.at[0], zs_sem.at[1], z=far),
        remote(zd_out, zd_in, zs_sem.at[2], zs_sem.at[3], z=far),
    ]
    starts(zs)

    @pl.loop(1, NCHIP)
    def _(k):
        r5_from(k).wait_recv()

    r6 = remote(out_r.at[c], out_r.at[c], r6_sem.at[0], r6_sem.at[1], c=other)
    r6.start()
    for cp in to_far + first + later + swap_p + swap_s + gates_p + gates_s + rows_p + rows_s:
        cp.wait_send()
    for m in range(2):
        half(m, c).wait_send()

    @pl.loop(1, NCHIP)
    def _(k):
        for m in range(2):
            plane_copy(m, k).wait_send()
        for cp in scatter(0, k, *arrays_p) + scatter(1, k, *arrays_s):
            cp.wait_send()
        for r in (r2, r3, r4, r5):
            r(k).wait_send()

    for cp in zs:
        cp.wait()
    out_w[...] += za_in[...].astype(F32)
    out_d[...] += zd_in[...].astype(F32)
    r6.wait_send()
    remote(out_r.at[other], out_r.at[other], r6_sem.at[0], r6_sem.at[1], c=other).wait_recv()


def local(tokens, grad_out, expert_ids, router_weight, wg, wu, wd):
    hbm = pl.BlockSpec(memory_space=pl.ANY)
    vmem = pl.BlockSpec(memory_space=pltpu.VMEM)
    dma = pltpu.SemaphoreType.DMA
    V = pltpu.VMEM
    blocks = [V((NCHIP, 32, 768), BF16), V((NCHIP, 16, 1024), BF16)]
    grad_tokens, grads, down, router = pl.pallas_call(
        whole,
        out_shape=(
            jax.ShapeDtypeStruct((256, 1024), BF16),
            jax.ShapeDtypeStruct((32, 768), F32),
            jax.ShapeDtypeStruct((16, 1024), F32),
            jax.ShapeDtypeStruct((2, 16, 16, 2, 128), F32),
        ),
        in_specs=[hbm] * 7,
        out_specs=(vmem,) * 4,
        scratch_shapes=[
            V((256, 1024), BF16), V((256, 1024), BF16), V((256, 8), jnp.int32), V((1024, 128), BF16),
            V((1024, 768), BF16), V((384, 1024), BF16), V((1024, 768), BF16), V((384, 1024), BF16),
            V((512, 256), BF16), V((256, 128), F32), V((16, CAP, 1024), BF16), V((16, CAP, 1024), BF16),
            V((NP, 8, 128), F32), V((384, 512), BF16),
            V((NP, CAP, 1024), BF16), V((NS, CAP, 1024), BF16), V((NP, CAP, 1024), BF16), V((NS, CAP, 1024), BF16),
            V((NP, 8, 128), F32),
            V((NP, CAP, 768), F32), V((NP, CAP, 384), F32), V((NP, CAP, 1024), BF16),
            V((NP, CAP, 768), BF16), V((NP, CAP, 384), BF16), V((NP, CAP, 1024), F32),
            V((NP, CAP, 1024), BF16), V((NS, CAP, 1024), BF16), V((NP, 2, 1, 128), F32),
            V((16, CAP, 1024), BF16), V((NP, 2, 1, 128), F32), V((512, 128), BF16),
            V((16, 2, 32, 768), BF16), V((16, 2, 16, 1024), BF16),
            V((16, 2, 32, 768), BF16), V((16, 2, 16, 1024), BF16),
            *blocks, *blocks, *blocks, *blocks, *blocks, *blocks,
            V((32, 768), BF16), V((16, 1024), BF16), V((32, 768), BF16), V((16, 1024), BF16),
            V((2, 16, 16, 2, 128), F32), V((16, 16, 2, 128), F32), V((16, 16, 2, 128), F32),
            V((16, 16, 2, 128), F32), V((16, 2, 128), F32), V((16, 2, 128), F32),
            dma((7,)), dma((16,)), dma((16,)), dma((16,)), dma((16,)), dma((9,)), dma((9,)),
            dma((2,)), dma((2,)), dma((2, 16)), dma((2, 16)), dma((2,)), dma((2,)),
            dma((16,)), dma((16,)), dma((2, 9)), dma((2, 9)),
            dma((2, 2)), dma((2, 2)), dma((2, 2, 16)), dma((2, 2, 16)), dma((4,)),
            dma((2,)), dma((16,)), dma((16,)), dma((16,)), dma((16,)), dma((16,)), dma((16,)),
            dma((16,)), dma((16,)), dma((2,)),
        ],
        compiler_params=pltpu.CompilerParams(
            collective_id=0, has_side_effects=True, vmem_limit_bytes=58 << 20
        ),
        name="whole",
    )(tokens, grad_out, expert_ids, router_weight, wg[0], wu[0], wd[0])
    return (
        grad_tokens,
        grads[None, :, :384],
        grads[None, :, 384:],
        down[None, :12],
        router.reshape(1024, 128),
    )


def solution(mesh):
    finer = Mesh(mesh.devices.reshape(4, 4, 2, NZ), AX)
    dp = AX[:3]
    return jax.shard_map(
        local,
        mesh=finer,
        in_specs=(
            P(AX, None), P(AX, None), P(AX, None), P(),
            P("expert", None, None), P("expert", None, None), P("expert", None, None),
        ),
        out_specs=(
            P(AX, None), P("expert", dp, None), P("expert", dp, None), P("expert", dp, None), P(),
        ),
        check_vma=False,
    )
```

time: 203 us -> 147 us (0.72)
  the two profiles are of different devices: /device:TPU:60 before, /device:TPU:39 now
where the time goes in v2:
time: 147 us
  Pallas kernels  140 us (95%)
  local copies, waits for them, and re-layouts  6.4 us (4%)
    pallas_call x1, Pallas kernels, local(): pl.pallas_call(whole, out_shape=(jax.ShapeDtypeStruct((256, 1024), BF16),...  140 us
    unnamed x8, local copies, waits for them, and re-layouts  4.88 us

profile of v2, /device:TPU:39, one launch (start us, length us, event | category | flops | bytes accessed | tf_op | source)
XLA Modules:
  0.0 147.3 jit_solution(9997071974622715380)
XLA Ops:
  0.6 1.5 %copy.12.ids_h = s32[256,8]{1,0:T(8,128)} copy(s32[256,8]{0,1:T(8,128)} %param.9) | data formatting | bytes 16384 | tf_op args[2]
  2.1 140.2 %whole.1 = (bf16[256,1024]{1,0:T(8,128)(2,1)}, f32[32,768]{1,0:T(8,128)}, f32[16,1024]{1,0:T(8,128)}, f32[2,16,16,2,128]{4,3,2,1,0:T(2,128)}) custom-call(bf16[256,1024]{1,0:T(8,128)(2,1)} %tok_h.1, bf16[256,1024]{1,0:T(8,128)(2,1)} %grad_h.1, s32[256,8]{1,0:T(8,128)} %copy.12.ids_h, bf16[1024,128]{1,0:T(8,128)(2,1)} %rw_h.1, bf16[1024,384]{1,0:T(8,128)(2,1)} %bitcast.10, ...), custom_call_target="tpu_custom_call" | custom-call | tf_op jit(solution)/shard_map/whole/pallas_call | solution.py:491
  142.4 0.0 copy-start.1
  142.4 0.9 slice_bitcast_fusion
  143.2 0.7 copy.13
  143.9 0.0 copy-done.1
  143.9 0.6 slice_bitcast_fusion.1
  144.6 0.0 copy-start
  144.6 1.9 %copy.16 = bf16[256,1024]{1,0:T(8,128)(2,1)} copy(bf16[256,1024]{1,0:T(8,128)(2,1)} %get-tuple-element.25) | data formatting | bytes 1048576
  146.5 0.0 copy-done
  146.5 0.8 copy.17
Async XLA Ops:
  142.4 1.6 %copy-start.1 = (f32[32,768]{1,0:T(8,128)S(1)}, f32[32,768]{1,0:T(8,128)}, u32[]{:S(2)}) copy-start(f32[32,768]{1,0:T(8,128)} %get-tuple-element.10) | copy-start | bytes 294916
  144.6 1.9 %copy-start = (f32[2,16,16,2,128]{4,3,2,1,0:T(2,128)S(1)}, f32[2,16,16,2,128]{4,3,2,1,0:T(2,128)}, u32[]{:S(2)}) copy-start(f32[2,16,16,2,128]{4,3,2,1,0:T(2,128)} %get-tuple-element.12) | copy-start | bytes 1572868

commit v3 on v2

--- a/solution.py
+++ b/solution.py
@@ -18,6 +18,7 @@
 NP, NS = 9, 7
 HOME = 3
 ORDER = (7, 8, 0, 6, 1, 5, 2, 4)
+NDP = 32
 
 
 def wrap(v, n):
@@ -45,7 +46,7 @@
 
 def whole(
     tok_h, grad_h, ids_h, rw_h, wg_h, wu_h, wd_h,
-    out_tok, out_w, out_d, out_r,
+    out_tok, out_g, out_u, out_d, out_r,
     tok, grad, ids, rw, w1, w1d, w2, w2d,
     oh, prob, st, sg, sgt, sel,
     ptok, stok, pgrad, sgrad, gts,
@@ -54,12 +55,12 @@
     pa, pd, sa, sd, sib_pa, sib_pd, sib_sa, sib_sd,
     s_pa, s_pd, s_sa, s_sd, rb_pa, rb_pd, rb_sa, rb_sd,
     za_out, zd_out, za_in, zd_in,
-    part, r_sib, r_half, r_in, r_z, r_zin,
+    total_d, part, r_in, r_zin, r_out,
     loc, t_send, t_recv, g_send, g_recv, gt_send, gt_recv,
     wz_send, wz_recv, wp_send, wp_recv, wc_send, wc_recv,
     row_send, row_recv, gg_send, gg_recv,
     sib_send, sib_recv, rs_send, rs_recv, zs_sem,
-    r1_sem, r2_send, r2_recv, r3_send, r3_recv, r4_send, r4_recv, r5_send, r5_recv, r6_sem,
+    r2_send, r2_recv, r3_send, r3_recv, r5_send, r5_recv,
 ):
     x, y, c, z = tuple(lax.axis_index(a) for a in AX)
     me = x * 4 + y
@@ -78,10 +79,17 @@
     starts(fetch)
 
     barrier = pltpu.get_barrier_semaphore()
-    partners = [dict(z=wrap(z + d, NZ)) for d in range(1, NZ)] + [dict(c=other)]
-    partners += [
-        dict(x=wrap(x + dx, 4), y=wrap(y + dy, 4)) for dx in range(4) for dy in range(4) if dx or dy
-    ]
+    mine32 = me * 2 + c
+
+    def plane(k):
+        to = wrap(mine32 + k, NDP)
+        return to, dict(x=to // 8, y=lax.rem(to // 2, 4), c=lax.rem(to, 2))
+
+    def plane_back(k):
+        frm = wrap(mine32 - k + NDP, NDP)
+        return frm, dict(x=frm // 8, y=lax.rem(frm // 2, 4), c=lax.rem(frm, 2))
+
+    partners = [dict(z=wrap(z + d, NZ)) for d in range(1, NZ)] + [plane(k)[1] for k in range(1, NDP)]
     for where in partners:
         pl.semaphore_signal(barrier, inc=1, device_id=at(where), device_id_type=MESH)
 
@@ -106,17 +114,19 @@
         return jnp.sum(jnp.where(lane == sub, row, 0.0), axis=1, keepdims=True)
 
     fetch[0].wait()
-    every = lax.broadcasted_iota(jnp.int32, (256, 128), 1)
-    named = ids[:, 0:1] == every
+    every = lax.broadcasted_iota(jnp.int32, (128, 256), 0)
+    names = ids[0:1, :] == every
     for k in range(1, 8):
-        named = jnp.logical_or(named, ids[:, k : k + 1] == every)
-    mask = jnp.where(named, 1.0, 0.0).astype(BF16)
+        names = jnp.logical_or(names, ids[k : k + 1, :] == every)
+    mask = jnp.where(names, 1.0, 0.0).astype(BF16)
+    unit = lax.broadcasted_iota(jnp.int32, (128, 128), 0) == lax.broadcasted_iota(jnp.int32, (128, 128), 1)
+    named = dot(mask, jnp.where(unit, 1.0, 0.0).astype(BF16), 0, 0) > 0.5
     row16 = lax.broadcasted_iota(jnp.int32, (16, 128), 0)
     rel = jnp.zeros((16, 128), jnp.int32)
     for g in range(16):
         rel = jnp.where(row16 == g, expert_of(g), rel)
     mine = jnp.where(lax.broadcasted_iota(jnp.int32, (16, 128), 1) == rel, 1.0, 0.0).astype(BF16)
-    served = dot(mine, mask, 1, 1)
+    served = dot(mine, mask, 1, 0)
     before = lax.broadcasted_iota(jnp.int32, (256, 256), 0) < lax.broadcasted_iota(jnp.int32, (256, 256), 1)
     rank = dot(served.astype(BF16), jnp.where(before, 1.0, 0.0).astype(BF16), 1, 0)
     slot = jnp.where(served > 0.5, rank, -1.0)
@@ -162,12 +172,12 @@
     for i in ORDER:
         to = wrap(z + DIST[i], NZ)
         first.append(remote(sgt.at[i], gts.at[i], gt_send.at[i], gt_recv.at[i], z=to))
-        first.append(remote(st.at[i], ptok.at[i], t_send.at[i], t_recv.at[i], z=to))
-        first.append(remote(sg.at[i], pgrad.at[i], g_send.at[i], g_recv.at[i], z=to))
+        later.append(remote(st.at[i], ptok.at[i], t_send.at[i], t_recv.at[i], z=to))
+        later.append(remote(sg.at[i], pgrad.at[i], g_send.at[i], g_recv.at[i], z=to))
         if i < NS:
             j = NP + i
-            later.append(remote(st.at[j], stok.at[i], t_send.at[j], t_recv.at[j], z=to))
-            later.append(remote(sg.at[j], sgrad.at[i], g_send.at[j], g_recv.at[j], z=to))
+            first.append(remote(st.at[j], stok.at[i], t_send.at[j], t_recv.at[j], z=to))
+            first.append(remote(sg.at[j], sgrad.at[i], g_send.at[j], g_recv.at[j], z=to))
     starts(first)
     starts(later)
     gts[HOME] = sgt[HOME]
@@ -289,48 +299,48 @@
             remote(s_d.at[0], rb_d.at[frm], rs_send.at[e, 1, k], rs_recv.at[e, 1, k], **where),
         ]
 
+    for m in range(2):
+        half(m, other).wait_recv()
     for cp in first:
         cp.wait_recv()
+    expert_rows(NS, stok, sgrad, 1, w2, w2d)
+    expert_parts(NS, stok, sa, sd)
+    swap_s = swap_core(sa, sd, sib_sa, sib_sd, 1)
+    starts(swap_s)
+    expert_gates(NS, sgrad, 1, w2d)
+    gates_s = give_gates(1, NS)
+    starts(gates_s)
+    expert_back(NS, w2, srow)
+    rows_s = give_rows(srow, NS, NP)
+    starts(rows_s)
+    rows_in[NP + HOME] = srow[HOME]
+    gg_in[HOME, 1] = gg[HOME, 1]
+    for cp in swap_s:
+        cp.wait_recv()
+    add_core(sa, sd, sib_sa, sib_sd, s_sa, s_sd)
+    arrays_s = (s_sa, s_sd, rb_sa, rb_sd)
+
+    @pl.loop(1, NCHIP)
+    def _(k):
+        starts(scatter(1, k, *arrays_s))
+
+    rb_sa[me] = s_sa[me]
+    rb_sd[me] = s_sd[me]
+
+    for cp in later:
+        cp.wait_recv()
     expert_rows(NP, ptok, pgrad, 0, w1, w1d)
+    expert_gates(NP, pgrad, 0, w1d)
+    gates_p = give_gates(0, NP)
+    starts(gates_p)
     expert_parts(NP, ptok, pa, pd)
     swap_p = swap_core(pa, pd, sib_pa, sib_pd, 0)
     starts(swap_p)
-    expert_gates(NP, pgrad, 0, w1d)
-    gates_p = give_gates(0, NP)
-    starts(gates_p)
     expert_back(NP, w1, prow)
     rows_p = give_rows(prow, NP, 0)
     starts(rows_p)
     rows_in[HOME] = prow[HOME]
     gg_in[HOME, 0] = gg[HOME, 0]
-    for cp in swap_p:
-        cp.wait_recv()
-    add_core(pa, pd, sib_pa, sib_pd, s_pa, s_pd)
-    arrays_p = (s_pa, s_pd, rb_pa, rb_pd)
-
-    @pl.loop(1, NCHIP)
-    def _(k):
-        starts(scatter(0, k, *arrays_p))
-
-    rb_pa[me] = s_pa[me]
-    rb_pd[me] = s_pd[me]
-
-    for m in range(2):
-        half(m, other).wait_recv()
-    for cp in later:
-        cp.wait_recv()
-    expert_rows(NS, stok, sgrad, 1, w2, w2d)
-    expert_gates(NS, sgrad, 1, w2d)
-    gates_s = give_gates(1, NS)
-    starts(gates_s)
-    expert_parts(NS, stok, sa, sd)
-    swap_s = swap_core(sa, sd, sib_sa, sib_sd, 1)
-    starts(swap_s)
-    expert_back(NS, w2, srow)
-    rows_s = give_rows(srow, NS, NP)
-    starts(rows_s)
-    rows_in[NP + HOME] = srow[HOME]
-    gg_in[HOME, 1] = gg[HOME, 1]
 
     for cp in gates_p + gates_s:
         cp.wait_recv()
@@ -341,125 +351,99 @@
     grads = dot(oh[...], vbuf[...], 0, 0)
     p = prob[...]
     logit_grad = (p * (grads - jnp.sum(p * grads, axis=1, keepdims=True))).astype(BF16)
-    part[...] = dot(tok[...], logit_grad, 0, 0).reshape(part.shape)
-    r1 = remote(part.at[other], r_sib, r1_sem.at[0], r1_sem.at[1], c=other)
-    r1.start()
-    for cp in swap_s:
-        cp.wait_recv()
-    add_core(sa, sd, sib_sa, sib_sd, s_sa, s_sd)
-    arrays_s = (s_sa, s_sd, rb_sa, rb_sd)
-    r1.wait()
-    r_half[...] = part[c] + r_sib[...]
-    r_in[me] = r_half[me]
+    part[...] = dot(tok[...], logit_grad, 0, 0).astype(BF16).reshape(part.shape)
 
     def r2(k):
-        to, where = chip(k)
-        return remote(r_half.at[to], r_in.at[me], r2_send.at[k], r2_recv.at[k], **where)
+        to, where = plane(k)
+        return remote(part.at[to], r_in.at[mine32], r2_send.at[k], r2_recv.at[k], **where)
 
     def r2_from(k):
-        frm, where = chip_from(k)
-        return remote(r_half.at[0], r_in.at[frm], r2_send.at[k], r2_recv.at[k], **where)
-
-    @pl.loop(1, NCHIP)
+        frm, where = plane_back(k)
+        return remote(part.at[0], r_in.at[frm], r2_send.at[k], r2_recv.at[k], **where)
+
+    @pl.loop(1, NDP)
     def _(k):
         r2(k).start()
 
-    @pl.loop(1, NCHIP)
-    def _(k):
-        starts(scatter(1, k, *arrays_s))
-
-    rb_sa[me] = s_sa[me]
-    rb_sd[me] = s_sd[me]
-
-    @pl.loop(1, NCHIP)
+    r_in[mine32] = part[mine32]
+    for cp in swap_p:
+        cp.wait_recv()
+    add_core(pa, pd, sib_pa, sib_pd, s_pa, s_pd)
+    arrays_p = (s_pa, s_pd, rb_pa, rb_pd)
+
+    @pl.loop(1, NCHIP)
+    def _(k):
+        starts(scatter(0, k, *arrays_p))
+
+    rb_pa[me] = s_pa[me]
+    rb_pd[me] = s_pd[me]
+
+    @pl.loop(1, NCHIP)
+    def _(k):
+        for cp in scattered(1, k, *arrays_s):
+            cp.wait_recv()
+
+    za_out[...] = jnp.sum(rb_sa[...].astype(F32), axis=0).astype(BF16)
+    zd_out[...] = jnp.sum(rb_sd[...].astype(F32), axis=0).astype(BF16)
+
+    @pl.loop(1, NDP)
     def _(k):
         r2_from(k).wait_recv()
 
-    r_z[...] = jnp.sum(r_in[...], axis=0)
+    r_zin[z] = jnp.sum(r_in[...].astype(F32), axis=0).astype(BF16)
 
     def r3(k):
-        return remote(r_z.at[wrap(z + k, NZ)], r_zin.at[z], r3_send.at[k], r3_recv.at[k], z=wrap(z + k, NZ))
+        return remote(r_zin.at[z], r_zin.at[z], r3_send.at[k], r3_recv.at[k], z=wrap(z + k, NZ))
 
     def r3_from(k):
         frm = wrap(z - k + NZ, NZ)
-        return remote(r_z.at[0], r_zin.at[frm], r3_send.at[k], r3_recv.at[k], z=frm)
+        return remote(r_zin.at[frm], r_zin.at[frm], r3_send.at[k], r3_recv.at[k], z=frm)
 
     @pl.loop(1, NZ)
     def _(k):
         r3(k).start()
 
-    r_zin[z] = r_z[z]
-
-    for cp in rows_p + rows_s:
-        cp.wait_recv()
-    out_tok[...] = (
-        dot(oh[...], rows_in[...].reshape(512, 1024), 0, 0) + dot(logit_grad, rw[...], 1, 1)
-    ).astype(BF16)
-
-    @pl.loop(1, NZ)
-    def _(k):
-        r3_from(k).wait_recv()
-
-    out_r[c, me, z] = jnp.sum(r_zin[...], axis=0)
-
-    def r4(k):
-        ref = out_r.at[c, me, z]
-        return remote(ref, ref, r4_send.at[k], r4_recv.at[k], z=wrap(z + k, NZ))
-
-    def r4_from(k):
-        frm = wrap(z - k + NZ, NZ)
-        ref = out_r.at[c, me, frm]
-        return remote(ref, ref, r4_send.at[k], r4_recv.at[k], z=frm)
-
-    @pl.loop(1, NZ)
-    def _(k):
-        r4(k).start()
-
-    @pl.loop(1, NCHIP)
-    def _(k):
-        for cp in scattered(0, k, *arrays_p):
-            cp.wait_recv()
-
-    out_w[...] = jnp.sum(rb_pa[...].astype(F32), axis=0)
-    out_d[...] = jnp.sum(rb_pd[...].astype(F32), axis=0)
-
-    @pl.loop(1, NZ)
-    def _(k):
-        r4_from(k).wait_recv()
-
-    def r5(k):
-        _to, where = chip(k)
-        ref = out_r.at[c, me]
-        return remote(ref, ref, r5_send.at[k], r5_recv.at[k], **where)
-
-    def r5_from(k):
-        frm, where = chip_from(k)
-        ref = out_r.at[c, frm]
-        return remote(ref, ref, r5_send.at[k], r5_recv.at[k], **where)
-
-    @pl.loop(1, NCHIP)
-    def _(k):
-        r5(k).start()
-
-    @pl.loop(1, NCHIP)
-    def _(k):
-        for cp in scattered(1, k, *arrays_s):
-            cp.wait_recv()
-
-    za_out[...] = jnp.sum(rb_sa[...].astype(F32), axis=0).astype(BF16)
-    zd_out[...] = jnp.sum(rb_sd[...].astype(F32), axis=0).astype(BF16)
     zs = [
         remote(za_out, za_in, zs_sem.at[0], zs_sem.at[1], z=far),
         remote(zd_out, zd_in, zs_sem.at[2], zs_sem.at[3], z=far),
     ]
     starts(zs)
 
-    @pl.loop(1, NCHIP)
-    def _(k):
-        r5_from(k).wait_recv()
-
-    r6 = remote(out_r.at[c], out_r.at[c], r6_sem.at[0], r6_sem.at[1], c=other)
-    r6.start()
+    for cp in rows_p + rows_s:
+        cp.wait_recv()
+    out_tok[...] = (
+        dot(oh[...], rows_in[...].reshape(512, 1024), 0, 0) + dot(logit_grad, rw[...], 1, 1)
+    ).astype(BF16)
+
+    @pl.loop(1, NZ)
+    def _(k):
+        r3_from(k).wait_recv()
+
+    r_out[mine32] = jnp.sum(r_zin[...].astype(F32), axis=0).astype(BF16)
+
+    def r5(k):
+        ref = r_out.at[mine32]
+        return remote(ref, ref, r5_send.at[k], r5_recv.at[k], **plane(k)[1])
+
+    def r5_from(k):
+        frm, where = plane_back(k)
+        ref = r_out.at[frm]
+        return remote(ref, ref, r5_send.at[k], r5_recv.at[k], **where)
+
+    @pl.loop(1, NDP)
+    def _(k):
+        r5(k).start()
+
+    @pl.loop(1, NCHIP)
+    def _(k):
+        for cp in scattered(0, k, *arrays_p):
+            cp.wait_recv()
+
+    total = jnp.sum(rb_pa[...].astype(F32), axis=0)
+    out_g[...] = total[:, :384]
+    out_u[...] = total[:, 384:]
+    total_d[...] = jnp.sum(rb_pd[...].astype(F32), axis=0)
+
     for cp in to_far + first + later + swap_p + swap_s + gates_p + gates_s + rows_p + rows_s:
         cp.wait_send()
     for m in range(2):
@@ -471,15 +455,26 @@
             plane_copy(m, k).wait_send()
         for cp in scatter(0, k, *arrays_p) + scatter(1, k, *arrays_s):
             cp.wait_send()
-        for r in (r2, r3, r4, r5):
-            r(k).wait_send()
+        r3(k).wait_send()
+
+    @pl.loop(1, NDP)
+    def _(k):
+        r2(k).wait_send()
+        r5(k).wait_send()
 
     for cp in zs:
         cp.wait()
-    out_w[...] += za_in[...].astype(F32)
-    out_d[...] += zd_in[...].astype(F32)
-    r6.wait_send()
-    remote(out_r.at[other], out_r.at[other], r6_sem.at[0], r6_sem.at[1], c=other).wait_recv()
+    out_g[...] += za_in[:, :384].astype(F32)
+    out_u[...] += za_in[:, 384:].astype(F32)
+    total_d[...] += zd_in[...].astype(F32)
+    for n in range(8):
+        out_d[:, n, :] = total_d[0:12, n * 128 : (n + 1) * 128]
+
+    @pl.loop(1, NDP)
+    def _(k):
+        r5_from(k).wait_recv()
+
+    out_r[...] = r_out[...].reshape(1024, 128).astype(F32)
 
 
 def local(tokens, grad_out, expert_ids, router_weight, wg, wu, wd):
@@ -488,18 +483,19 @@
     dma = pltpu.SemaphoreType.DMA
     V = pltpu.VMEM
     blocks = [V((NCHIP, 32, 768), BF16), V((NCHIP, 16, 1024), BF16)]
-    grad_tokens, grads, down, router = pl.pallas_call(
+    grad_tokens, gate, up, down, router = pl.pallas_call(
         whole,
         out_shape=(
             jax.ShapeDtypeStruct((256, 1024), BF16),
-            jax.ShapeDtypeStruct((32, 768), F32),
-            jax.ShapeDtypeStruct((16, 1024), F32),
-            jax.ShapeDtypeStruct((2, 16, 16, 2, 128), F32),
+            jax.ShapeDtypeStruct((32, 384), F32),
+            jax.ShapeDtypeStruct((32, 384), F32),
+            jax.ShapeDtypeStruct((12, 8, 128), F32),
+            jax.ShapeDtypeStruct((1024, 128), F32),
         ),
         in_specs=[hbm] * 7,
-        out_specs=(vmem,) * 4,
+        out_specs=(vmem,) * 5,
         scratch_shapes=[
-            V((256, 1024), BF16), V((256, 1024), BF16), V((256, 8), jnp.int32), V((1024, 128), BF16),
+            V((256, 1024), BF16), V((256, 1024), BF16), V((8, 256), jnp.int32), V((1024, 128), BF16),
             V((1024, 768), BF16), V((384, 1024), BF16), V((1024, 768), BF16), V((384, 1024), BF16),
             V((512, 256), BF16), V((256, 128), F32), V((16, CAP, 1024), BF16), V((16, CAP, 1024), BF16),
             V((NP, 8, 128), F32), V((384, 512), BF16),
@@ -513,26 +509,25 @@
             V((16, 2, 32, 768), BF16), V((16, 2, 16, 1024), BF16),
             *blocks, *blocks, *blocks, *blocks, *blocks, *blocks,
             V((32, 768), BF16), V((16, 1024), BF16), V((32, 768), BF16), V((16, 1024), BF16),
-            V((2, 16, 16, 2, 128), F32), V((16, 16, 2, 128), F32), V((16, 16, 2, 128), F32),
-            V((16, 16, 2, 128), F32), V((16, 2, 128), F32), V((16, 2, 128), F32),
+            V((16, 1024), F32), V((NDP, 32, 128), BF16), V((NDP, 32, 128), BF16),
+            V((NZ, 32, 128), BF16), V((NDP, 32, 128), BF16),
             dma((7,)), dma((16,)), dma((16,)), dma((16,)), dma((16,)), dma((9,)), dma((9,)),
             dma((2,)), dma((2,)), dma((2, 16)), dma((2, 16)), dma((2,)), dma((2,)),
             dma((16,)), dma((16,)), dma((2, 9)), dma((2, 9)),
             dma((2, 2)), dma((2, 2)), dma((2, 2, 16)), dma((2, 2, 16)), dma((4,)),
-            dma((2,)), dma((16,)), dma((16,)), dma((16,)), dma((16,)), dma((16,)), dma((16,)),
-            dma((16,)), dma((16,)), dma((2,)),
+            dma((NDP,)), dma((NDP,)), dma((16,)), dma((16,)), dma((NDP,)), dma((NDP,)),
         ],
         compiler_params=pltpu.CompilerParams(
-            collective_id=0, has_side_effects=True, vmem_limit_bytes=58 << 20
+            collective_id=0, has_side_effects=True, vmem_limit_bytes=52 << 20
         ),
         name="whole",
-    )(tokens, grad_out, expert_ids, router_weight, wg[0], wu[0], wd[0])
+    )(tokens, grad_out, expert_ids.T, router_weight, wg[0], wu[0], wd[0])
     return (
         grad_tokens,
-        grads[None, :, :384],
-        grads[None, :, 384:],
-        down[None, :12],
-        router.reshape(1024, 128),
+        gate[None],
+        up[None],
+        down.reshape(1, 12, 1024),
+        router,
     )
 
 

time: 147 us -> 136 us (0.925)
  the two profiles are of different devices: /device:TPU:39 before, /device:TPU:1 now
where the time goes in v3:
time: 136 us
  Pallas kernels  129 us (95%)
  local copies, waits for them, and re-layouts  6.13 us (5%)
    pallas_call x1, Pallas kernels, local(): pl.pallas_call(whole, out_shape=(jax.ShapeDtypeStruct((256, 1024), BF16),...  129 us
    unnamed x11, local copies, waits for them, and re-layouts  6.13 us

profile of v3, /device:TPU:1, one launch (start us, length us, event | category | flops | bytes accessed | tf_op | source)
XLA Modules:
  0.0 136.2 jit_solution(10144560826871014493)
XLA Ops:
  0.6 0.0 copy-start
  0.6 1.0 copy-done
  1.7 0.0 copy-start.1
  1.7 0.9 copy-done.1
  2.6 0.0 copy-start.2
  2.6 0.7 copy-done.2
  3.3 129.4 %whole.1 = (bf16[256,1024]{1,0:T(8,128)(2,1)S(1)}, f32[32,384]{1,0:T(8,128)S(1)}, f32[32,384]{1,0:T(8,128)S(1)}, f32[12,8,128]{2,1,0:T(8,128)S(1)}, f32[1024,128]{1,0:T(8,128)S(1)}) custom-call(bf16[256,1024]{1,0:T(8,128)(2,1)S(1)} %copy-done, bf16[256,1024]{1,0:T(8,128)(2,1)} %grad_h.1, s32[8,256]{1,0:T(8,128)S(1)} %bitcast.10, ...), custom_call_target="tpu_custom_call" | custom-call | tf_op jit(solution)/shard_map/whole/pallas_call | solution.py:486
  132.8 0.8 copy.19
  133.6 0.6 copy.20
  134.2 0.6 copy.21
  134.8 0.6 copy.22
  135.4 0.8 copy.23
Async XLA Ops:
  0.6 1.0 copy-start
  1.7 0.9 copy-start.1
  2.6 0.7 copy-start.2

commit v4 on v3

--- a/solution.py
+++ b/solution.py
@@ -56,11 +56,11 @@
     s_pa, s_pd, s_sa, s_sd, rb_pa, rb_pd, rb_sa, rb_sd,
     za_out, zd_out, za_in, zd_in,
     total_d, part, r_in, r_zin, r_out,
-    loc, t_send, t_recv, g_send, g_recv, gt_send, gt_recv,
+    loc, row_sem, gt_sem,
     wz_send, wz_recv, wp_send, wp_recv, wc_send, wc_recv,
-    row_send, row_recv, gg_send, gg_recv,
+    back_send, back_recv, gg_send, gg_recv,
     sib_send, sib_recv, rs_send, rs_recv, zs_sem,
-    r2_send, r2_recv, r3_send, r3_recv, r5_send, r5_recv,
+    r_sem,
 ):
     x, y, c, z = tuple(lax.axis_index(a) for a in AX)
     me = x * 4 + y
@@ -171,15 +171,30 @@
     first, later = [], []
     for i in ORDER:
         to = wrap(z + DIST[i], NZ)
-        first.append(remote(sgt.at[i], gts.at[i], gt_send.at[i], gt_recv.at[i], z=to))
-        later.append(remote(st.at[i], ptok.at[i], t_send.at[i], t_recv.at[i], z=to))
-        later.append(remote(sg.at[i], pgrad.at[i], g_send.at[i], g_recv.at[i], z=to))
+        first.append(remote(sgt.at[i], gts.at[i], gt_sem.at[0], gt_sem.at[1], z=to))
+        later.append(remote(st.at[i], ptok.at[i], row_sem.at[0], row_sem.at[1], z=to))
+        later.append(remote(sg.at[i], pgrad.at[i], row_sem.at[2], row_sem.at[3], z=to))
         if i < NS:
             j = NP + i
-            first.append(remote(st.at[j], stok.at[i], t_send.at[j], t_recv.at[j], z=to))
-            first.append(remote(sg.at[j], sgrad.at[i], g_send.at[j], g_recv.at[j], z=to))
+            first.append(remote(st.at[j], stok.at[i], row_sem.at[4], row_sem.at[5], z=to))
+            first.append(remote(sg.at[j], sgrad.at[i], row_sem.at[6], row_sem.at[7], z=to))
     starts(first)
     starts(later)
+
+    def group(ref, n, send, recv):
+        refs = ref.at[pl.ds(0, n)]
+        return remote(refs, refs, send, recv, z=far)
+
+    gt_all = group(gts, NP - 1, gt_sem.at[0], gt_sem.at[1])
+    first_all = [
+        group(stok, NS - 1, row_sem.at[4], row_sem.at[5]),
+        group(sgrad, NS - 1, row_sem.at[6], row_sem.at[7]),
+        gt_all,
+    ]
+    later_all = [
+        group(ptok, NP - 1, row_sem.at[0], row_sem.at[1]),
+        group(pgrad, NP - 1, row_sem.at[2], row_sem.at[3]),
+    ]
     gts[HOME] = sgt[HOME]
     ptok[HOME] = st[HOME]
     pgrad[HOME] = sg[HOME]
@@ -197,22 +212,20 @@
     def plane_copy(m, k):
         _to, where = chip(k)
         mine_ = piece(second[m], m, c, me)
-        return remote(mine_, mine_, wp_send.at[m, k], wp_recv.at[m, k], **where)
-
-    def plane_from(m, k):
-        frm, where = chip_from(k)
-        theirs = piece(second[m], m, c, frm)
-        return remote(theirs, theirs, wp_send.at[m, k], wp_recv.at[m, k], **where)
+        return remote(mine_, mine_, wp_send.at[m], wp_recv.at[m], **where)
+
+    plane_all = [
+        remote(ref, ref, wp_send.at[m], wp_recv.at[m], c=other)
+        for m, ref in enumerate((w2.at[pl.ds(0, 480)], w2d.at[pl.ds(0, 240), pl.ds(0, 768)]))
+    ]
 
     @pl.loop(1, NCHIP)
     def _(k):
         for m in range(2):
             plane_copy(m, k).start()
 
-    @pl.loop(1, NCHIP)
-    def _(k):
-        for m in range(2):
-            plane_from(m, k).wait_recv()
+    for cp in plane_all:
+        cp.wait_recv()
 
     def half(m, core):
         n = 512 if m == 0 else 192
@@ -261,14 +274,14 @@
 
     def give_gates(s, n):
         return [
-            remote(gg.at[i, s], gg_in.at[i, s], gg_send.at[s, i], gg_recv.at[s, i], z=wrap(z - DIST[i] + NZ, NZ))
+            remote(gg.at[i, s], gg_in.at[i, s], gg_send.at[s], gg_recv.at[s], z=wrap(z - DIST[i] + NZ, NZ))
             for i in ORDER
             if i < n
         ]
 
     def give_rows(back, n, base):
         return [
-            remote(back.at[i], rows_in.at[base + i], row_send.at[base + i], row_recv.at[base + i], z=wrap(z - DIST[i] + NZ, NZ))
+            remote(back.at[i], rows_in.at[base + i], back_send.at[base // NP], back_recv.at[base // NP], z=wrap(z - DIST[i] + NZ, NZ))
             for i in ORDER
             if i < n
         ]
@@ -288,20 +301,19 @@
     def scatter(e, k, s_a, s_d, rb_a, rb_d):
         to, where = chip(k)
         return [
-            remote(s_a.at[to], rb_a.at[me], rs_send.at[e, 0, k], rs_recv.at[e, 0, k], **where),
-            remote(s_d.at[to], rb_d.at[me], rs_send.at[e, 1, k], rs_recv.at[e, 1, k], **where),
+            remote(s_a.at[to], rb_a.at[me], rs_send.at[e, 0], rs_recv.at[e, 0], **where),
+            remote(s_d.at[to], rb_d.at[me], rs_send.at[e, 1], rs_recv.at[e, 1], **where),
         ]
 
-    def scattered(e, k, s_a, s_d, rb_a, rb_d):
-        frm, where = chip_from(k)
+    def scattered_all(e, rb_a, rb_d):
         return [
-            remote(s_a.at[0], rb_a.at[frm], rs_send.at[e, 0, k], rs_recv.at[e, 0, k], **where),
-            remote(s_d.at[0], rb_d.at[frm], rs_send.at[e, 1, k], rs_recv.at[e, 1, k], **where),
+            group(rb_a, NCHIP - 1, rs_send.at[e, 0], rs_recv.at[e, 0]),
+            group(rb_d, NCHIP - 1, rs_send.at[e, 1], rs_recv.at[e, 1]),
         ]
 
     for m in range(2):
         half(m, other).wait_recv()
-    for cp in first:
+    for cp in first_all:
         cp.wait_recv()
     expert_rows(NS, stok, sgrad, 1, w2, w2d)
     expert_parts(NS, stok, sa, sd)
@@ -327,12 +339,21 @@
     rb_sa[me] = s_sa[me]
     rb_sd[me] = s_sd[me]
 
-    for cp in later:
+    for cp in scattered_all(1, rb_sa, rb_sd):
+        cp.wait_recv()
+    za_out[...] = jnp.sum(rb_sa[...].astype(F32), axis=0).astype(BF16)
+    zd_out[...] = jnp.sum(rb_sd[...].astype(F32), axis=0).astype(BF16)
+    for cp in later_all:
         cp.wait_recv()
     expert_rows(NP, ptok, pgrad, 0, w1, w1d)
     expert_gates(NP, pgrad, 0, w1d)
     gates_p = give_gates(0, NP)
     starts(gates_p)
+    zs = [
+        remote(za_out, za_in, zs_sem.at[0], zs_sem.at[1], z=far),
+        remote(zd_out, zd_in, zs_sem.at[2], zs_sem.at[3], z=far),
+    ]
+    starts(zs)
     expert_parts(NP, ptok, pa, pd)
     swap_p = swap_core(pa, pd, sib_pa, sib_pd, 0)
     starts(swap_p)
@@ -342,7 +363,8 @@
     rows_in[HOME] = prow[HOME]
     gg_in[HOME, 0] = gg[HOME, 0]
 
-    for cp in gates_p + gates_s:
+    gates_all = [group(gg_in.at[:, s], n - 1, gg_send.at[s], gg_recv.at[s]) for s, n in enumerate((NP, NS))]
+    for cp in gates_all:
         cp.wait_recv()
     for g in range(16):
         i, s = (g, 0) if g < NP else (g - NP, 1)
@@ -355,11 +377,9 @@
 
     def r2(k):
         to, where = plane(k)
-        return remote(part.at[to], r_in.at[mine32], r2_send.at[k], r2_recv.at[k], **where)
-
-    def r2_from(k):
-        frm, where = plane_back(k)
-        return remote(part.at[0], r_in.at[frm], r2_send.at[k], r2_recv.at[k], **where)
+        return remote(part.at[to], r_in.at[mine32], r_sem.at[2, 0], r_sem.at[2, 1], **where)
+
+    r2_all = group(r_in, NDP - 1, r_sem.at[2, 0], r_sem.at[2, 1])
 
     @pl.loop(1, NDP)
     def _(k):
@@ -378,90 +398,54 @@
     rb_pa[me] = s_pa[me]
     rb_pd[me] = s_pd[me]
 
-    @pl.loop(1, NCHIP)
-    def _(k):
-        for cp in scattered(1, k, *arrays_s):
-            cp.wait_recv()
-
-    za_out[...] = jnp.sum(rb_sa[...].astype(F32), axis=0).astype(BF16)
-    zd_out[...] = jnp.sum(rb_sd[...].astype(F32), axis=0).astype(BF16)
-
-    @pl.loop(1, NDP)
-    def _(k):
-        r2_from(k).wait_recv()
+    r2_all.wait_recv()
 
     r_zin[z] = jnp.sum(r_in[...].astype(F32), axis=0).astype(BF16)
 
     def r3(k):
-        return remote(r_zin.at[z], r_zin.at[z], r3_send.at[k], r3_recv.at[k], z=wrap(z + k, NZ))
-
-    def r3_from(k):
-        frm = wrap(z - k + NZ, NZ)
-        return remote(r_zin.at[frm], r_zin.at[frm], r3_send.at[k], r3_recv.at[k], z=frm)
+        return remote(r_zin.at[z], r_zin.at[z], r_sem.at[3, 0], r_sem.at[3, 1], z=wrap(z + k, NZ))
+
+    r3_all = group(r_zin, NZ - 1, r_sem.at[3, 0], r_sem.at[3, 1])
 
     @pl.loop(1, NZ)
     def _(k):
         r3(k).start()
 
-    zs = [
-        remote(za_out, za_in, zs_sem.at[0], zs_sem.at[1], z=far),
-        remote(zd_out, zd_in, zs_sem.at[2], zs_sem.at[3], z=far),
-    ]
-    starts(zs)
-
-    for cp in rows_p + rows_s:
+    rows_all = [group(rows_in, n - 1, back_send.at[e], back_recv.at[e]) for e, n in enumerate((NP, NS))]
+    for cp in rows_all:
         cp.wait_recv()
     out_tok[...] = (
         dot(oh[...], rows_in[...].reshape(512, 1024), 0, 0) + dot(logit_grad, rw[...], 1, 1)
     ).astype(BF16)
 
-    @pl.loop(1, NZ)
-    def _(k):
-        r3_from(k).wait_recv()
+    r3_all.wait_recv()
 
     r_out[mine32] = jnp.sum(r_zin[...].astype(F32), axis=0).astype(BF16)
 
     def r5(k):
         ref = r_out.at[mine32]
-        return remote(ref, ref, r5_send.at[k], r5_recv.at[k], **plane(k)[1])
-
-    def r5_from(k):
-        frm, where = plane_back(k)
-        ref = r_out.at[frm]
-        return remote(ref, ref, r5_send.at[k], r5_recv.at[k], **where)
+        return remote(ref, ref, r_sem.at[5, 0], r_sem.at[5, 1], **plane(k)[1])
+
+    r5_all = group(r_out, NDP - 1, r_sem.at[5, 0], r_sem.at[5, 1])
 
     @pl.loop(1, NDP)
     def _(k):
         r5(k).start()
 
-    @pl.loop(1, NCHIP)
-    def _(k):
-        for cp in scattered(0, k, *arrays_p):
-            cp.wait_recv()
+    for cp in scattered_all(0, rb_pa, rb_pd):
+        cp.wait_recv()
 
     total = jnp.sum(rb_pa[...].astype(F32), axis=0)
     out_g[...] = total[:, :384]
     out_u[...] = total[:, 384:]
     total_d[...] = jnp.sum(rb_pd[...].astype(F32), axis=0)
 
-    for cp in to_far + first + later + swap_p + swap_s + gates_p + gates_s + rows_p + rows_s:
+    for cp in to_far + first_all + later_all + swap_p + swap_s + gates_all + rows_all + plane_all:
+        cp.wait_send()
+    for cp in scattered_all(0, rb_pa, rb_pd) + scattered_all(1, rb_sa, rb_sd) + [r2_all, r3_all, r5_all]:
         cp.wait_send()
     for m in range(2):
         half(m, c).wait_send()
-
-    @pl.loop(1, NCHIP)
-    def _(k):
-        for m in range(2):
-            plane_copy(m, k).wait_send()
-        for cp in scatter(0, k, *arrays_p) + scatter(1, k, *arrays_s):
-            cp.wait_send()
-        r3(k).wait_send()
-
-    @pl.loop(1, NDP)
-    def _(k):
-        r2(k).wait_send()
-        r5(k).wait_send()
-
     for cp in zs:
         cp.wait()
     out_g[...] += za_in[:, :384].astype(F32)
@@ -470,15 +454,13 @@
     for n in range(8):
         out_d[:, n, :] = total_d[0:12, n * 128 : (n + 1) * 128]
 
-    @pl.loop(1, NDP)
-    def _(k):
-        r5_from(k).wait_recv()
+    r5_all.wait_recv()
 
     out_r[...] = r_out[...].reshape(1024, 128).astype(F32)
 
 
 def local(tokens, grad_out, expert_ids, router_weight, wg, wu, wd):
-    hbm = pl.BlockSpec(memory_space=pl.ANY)
+    hbm = pl.BlockSpec(memory_space=pltpu.HBM)
     vmem = pl.BlockSpec(memory_space=pltpu.VMEM)
     dma = pltpu.SemaphoreType.DMA
     V = pltpu.VMEM
@@ -511,17 +493,17 @@
             V((32, 768), BF16), V((16, 1024), BF16), V((32, 768), BF16), V((16, 1024), BF16),
             V((16, 1024), F32), V((NDP, 32, 128), BF16), V((NDP, 32, 128), BF16),
             V((NZ, 32, 128), BF16), V((NDP, 32, 128), BF16),
-            dma((7,)), dma((16,)), dma((16,)), dma((16,)), dma((16,)), dma((9,)), dma((9,)),
-            dma((2,)), dma((2,)), dma((2, 16)), dma((2, 16)), dma((2,)), dma((2,)),
-            dma((16,)), dma((16,)), dma((2, 9)), dma((2, 9)),
-            dma((2, 2)), dma((2, 2)), dma((2, 2, 16)), dma((2, 2, 16)), dma((4,)),
-            dma((NDP,)), dma((NDP,)), dma((16,)), dma((16,)), dma((NDP,)), dma((NDP,)),
+            dma((7,)), dma((8,)), dma((2,)),
+            dma((2,)), dma((2,)), dma((2,)), dma((2,)), dma((2,)), dma((2,)),
+            dma((2,)), dma((2,)), dma((2,)), dma((2,)),
+            dma((2, 2)), dma((2, 2)), dma((2, 2)), dma((2, 2)), dma((4,)),
+            dma((6, 2)),
         ],
         compiler_params=pltpu.CompilerParams(
             collective_id=0, has_side_effects=True, vmem_limit_bytes=52 << 20
         ),
         name="whole",
-    )(tokens, grad_out, expert_ids.T, router_weight, wg[0], wu[0], wd[0])
+    )(*(pltpu.with_memory_space_constraint(v, pltpu.HBM) for v in (tokens, grad_out, expert_ids.T, router_weight, wg[0], wu[0], wd[0])))
     return (
         grad_tokens,
         gate[None],

time: 136 us -> 120 us (0.88)
  Pallas kernels: 129 us -> 116 us
  local copies, waits for them, and re-layouts: 6.13 us -> 3.45 us
    pallas_call x1, Pallas kernels: 129 us -> 116 us  [local(): pl.pallas_call(whole, out_shape=(jax.ShapeDtypeStruct((256, 1024), BF16),...]
    unnamed x11 -> x5, local copies, waits for them, and re-layouts: 6.13 us -> 3.45 us
where the time goes in v4:
time: 120 us
  Pallas kernels  116 us (97%)
  local copies, waits for them, and re-layouts  3.45 us (3%)
    pallas_call x1, Pallas kernels, local(): pl.pallas_call(whole, out_shape=(jax.ShapeDtypeStruct((256, 1024), BF16),...  116 us
    unnamed x5, local copies, waits for them, and re-layouts  3.45 us

profile of v4, /device:TPU:1, one launch (start us, length us, event | category | flops | bytes accessed | tf_op | source)
XLA Modules:
  0.0 119.8 jit_solution(3596170186121938415)
XLA Ops:
  0.6 115.7 %whole.1 = (bf16[256,1024]{1,0:T(8,128)(2,1)S(1)}, f32[32,384]{1,0:T(8,128)S(1)}, f32[32,384]{1,0:T(8,128)S(1)}, f32[12,8,128]{2,1,0:T(8,128)S(1)}, f32[1024,128]{1,0:T(8,128)S(1)}) custom-call(bf16[256,1024]{1,0:T(8,128)(2,1)} %tok_h.1, bf16[256,1024]{1,0:T(8,128)(2,1)} %grad_h.1, s32[8,256]{1,0:T(8,128)} %bitcast.13, bf16[1024,128]{1,0:T(8,128)(2,1)} %rw_h.1, ...), custom_call_target="tpu_custom_call" | custom-call | tf_op jit(solution)/shard_map/whole/pallas_call | solution.py:468
  116.4 0.8 copy.19
  117.2 0.6 copy.20
  117.8 0.6 copy.21
  118.4 0.6 copy.22
  119.0 0.8 copy.23
